TPU v7x, 16 devices: a whole 2x2x2 slice. The times are simulated.
16 devices in a mesh: depth: 2 (over z), col: 2 (over y), row: 4 (over x, core).
Axes of the slice: x: 2, y: 2, z: 2, core: 2. Of those that a mesh axis runs over, the one named last changes fastest.
Arguments:
- tokens: bfloat16 [16384, 1024], P(('depth', 'row'), 'col')
- w_up: bfloat16 [1024, 4096], P('row', 'col')
- w_down: bfloat16 [4096, 1024], P('row', 'col')
- grad_out: bfloat16 [16384, 1024], P(('depth', 'row'), 'col')
Outputs:
- output 1: bfloat16 [16384, 1024], P(('depth', 'row'), 'col')
- output 2: bfloat16 [16384, 1024], P(('depth', 'row'), 'col')
- output 3: float32 [1024, 4096], P('row', 'col')
- output 4: float32 [4096, 1024], P('row', 'col')
All inputs are finite; a program needn't handle non-finite values.
Results may differ from a plain program's by a relative error of at most 0.001.
Values are sent between devices in bfloat16 or wider.
A program may use at most 1 GiB of HBM per device.

v0:
```python
import math
import jax
import jax.numpy as jnp
from jax import lax
from jax.sharding import PartitionSpec as P, NamedSharding

INV_ROOT_TWO = 1.0 / math.sqrt(2.0)
INV_ROOT_TAU = 1.0 / math.sqrt(2.0 * math.pi)


def gelu_value(pre_act):
    return 0.5 * pre_act * (1.0 + lax.erf(pre_act * INV_ROOT_TWO))


def gelu_slope(pre_act):
    return 0.5 * (1.0 + lax.erf(pre_act * INV_ROOT_TWO)) + pre_act * jnp.exp(-0.5 * pre_act * pre_act) * INV_ROOT_TAU


def solution(mesh):
    act_spec = P(("depth", "row"), "col")
    wgt_spec = P("row", "col")

    def grid_block(tok_blk, up_blk, down_blk, grad_blk):
        tok_rows = lax.all_gather(tok_blk, "col", axis=1, tiled=True)
        up_cols = lax.all_gather(up_blk, "row", axis=0, tiled=True)
        down_cols = lax.all_gather(down_blk, "row", axis=0, tiled=True)
        pre_act = jnp.einsum("th,hf->tf", tok_rows, up_cols, preferred_element_type=jnp.float32)
        hidden_act = gelu_value(pre_act).astype(jnp.bfloat16)
        act_rows = lax.all_gather(hidden_act, "col", axis=1, tiled=True)
        out_blk = jnp.einsum("tf,fh->th", act_rows, down_cols, preferred_element_type=jnp.float32).astype(jnp.bfloat16)
        act_part = jnp.einsum("th,fh->tf", grad_blk, down_cols, preferred_element_type=jnp.float32)
        grad_act = lax.psum_scatter(act_part, "col", scatter_dimension=1, tiled=True)
        grad_pre = (grad_act * gelu_slope(pre_act)).astype(jnp.bfloat16)
        tok_part = jnp.einsum("tf,hf->th", grad_pre, up_cols, preferred_element_type=jnp.float32)
        grad_tok = lax.psum_scatter(tok_part, "col", scatter_dimension=1, tiled=True).astype(jnp.bfloat16)
        down_part = jnp.einsum("tf,th->fh", act_rows, grad_blk, preferred_element_type=jnp.float32)
        down_sum = lax.psum(lax.psum_scatter(down_part, "row", scatter_dimension=0, tiled=True), "depth")
        up_part = jnp.einsum("th,tf->hf", tok_rows, grad_pre, preferred_element_type=jnp.float32)
        up_sum = lax.psum(lax.psum_scatter(up_part, "row", scatter_dimension=0, tiled=True), "depth")
        return out_blk, grad_tok, up_sum, down_sum

    return jax.shard_map(grid_block, mesh=mesh, in_specs=(act_spec, wgt_spec, wgt_spec, act_spec), out_specs=(act_spec, act_spec, wgt_spec, wgt_spec), check_vma=False)
```

profile of v0, /device:TPU:0, one launch (start us, length us, event | category | flops | bytes accessed | tf_op | source)
XLA Modules:
  0.0 1082.2 jit_solution(5368067267099459452)
XLA Ops:
  7.2 0.0 all-gather.11.cloned.1.call-start
  7.2 0.7 all-gather.11.cloned.1.call-update
  7.9 0.0 all-gather.5.cloned.1.call-start
  8.0 0.7 all-gather.5.cloned.1.call-update
  8.7 0.0 all-gather.7.cloned.1.call-start
  8.7 0.7 all-gather.7.cloned.1.call-update
  9.4 0.0 reduce-scatter.5.cloned.1.call-start
  9.4 35.4 %all-gather.11.cloned.1.call-done = bf16[4096,512]{1,0:T(8,128)(2,1)} async-done(((bf16[1024,512]{1,0:T(8,128)(2,1)}), bf16[4096,512]{1,0:T(8,128)(2,1)}) %all-gather.11.cloned.1.call-update) | async-done | bytes 4194320 | tf_op jit(solution)/shard_map/all_gather | solution.py:26
  44.8 16.7 %fusion.6 = f32[2048,4096]{1,0:T(8,128)} fusion(bf16[2048,512]{1,0:T(8,128)(2,1)S(1)} %copy-done, bf16[4096,512]{1,0:T(8,128)(2,1)} %all-gather.11.cloned.1.call-done), kind=kOutput, calls=%fused_computation.11 | convolution fusion | flops 8589934592 | bytes 39845888 | tf_op jit(solution)/shard_map/th,fh->tf/dot_general | solution.py:31
  61.5 0.0 reduce-scatter.5.cloned.1.call-update
  61.5 0.0 all-gather.9.cloned.1.call-start
  61.6 39.9 %all-gather.5.cloned.1.call-done = bf16[2048,1024]{1,0:T(8,128)(2,1)} async-done(((bf16[2048,512]{1,0:T(8,128)(2,1)}), bf16[2048,1024]{1,0:T(8,128)(2,1)}) %all-gather.5.cloned.1.call-update) | async-done | bytes 4194320 | tf_op jit(solution)/shard_map/all_gather | solution.py:24
  101.4 34.0 %all-gather.7.cloned.1.call-done = bf16[1024,2048]{1,0:T(8,128)(2,1)} async-done(((bf16[256,2048]{1,0:T(8,128)(2,1)}), bf16[1024,2048]{1,0:T(8,128)(2,1)}) %all-gather.7.cloned.1.call-update) | async-done | bytes 4194320 | tf_op jit(solution)/shard_map/all_gather | solution.py:25
  135.4 369.2 %reduce-scatter.5.cloned.1.call-done = f32[2048,2048]{1,0:T(8,128)} async-done(((f32[2048,4096]{1,0:T(8,128)}), f32[2048,2048]{1,0:T(8,128)}) %reduce-scatter.5.cloned.1.call-update) | async-done | bytes 16777232 | tf_op jit(solution)/shard_map/reduce_scatter | solution.py:32
  504.6 22.4 %fusion.5 = (bf16[2048,2048]{1,0:T(8,128)(2,1)}, bf16[2048,2048]{1,0:T(8,128)(2,1)}) fusion(f32[2048,2048]{1,0:T(8,128)} %reduce-scatter.5.cloned.1.call-done, bf16[2048,1024]{1,0:T(8,128)(2,1)} %all-gather.5.cloned.1.call-done, bf16[1024,2048]{1,0:T(8,128)(2,1)} %all-gather.7.cloned.1.call-done), kind=kOutput, calls=%fused_computation.6 | convolution fusion | flops 8644460544 | bytes 41943040 | tf_op jit(solution)/shard_map/th,hf->tf/dot_general | solution.py:27
  527.0 0.0 all-gather.9.cloned.1.call-update
  527.0 0.0 reduce-scatter.9.cloned.1.call-start
  527.1 14.6 %convolution_bitcast_fusion = f32[1024,2048]{0,1:T(8,128)} fusion(bf16[2048,2048]{1,0:T(8,128)(2,1)} %get-tuple-element.10, bf16[2048,1024]{1,0:T(8,128)(2,1)} %all-gather.5.cloned.1.call-done), kind=kOutput, calls=%fused_computation.9 | convolution fusion | flops 8589934592 | bytes 20971520 | tf_op jit(solution)/shard_map/th,tf->hf/dot_general | solution.py:38
  541.7 0.2 reduce-scatter.11.cloned.1.call-start
  541.9 182.9 %all-gather.9.cloned.1.call-done = bf16[2048,4096]{1,0:T(8,128)(2,1)} async-done(((bf16[2048,2048]{1,0:T(8,128)(2,1)}), bf16[2048,4096]{1,0:T(8,128)(2,1)}) %all-gather.9.cloned.1.call-update) | async-done | bytes 16777232 | tf_op jit(solution)/shard_map/all_gather | solution.py:29
  724.8 14.5 %fusion.8 = f32[4096,512]{1,0:T(8,128)} fusion(bf16[2048,4096]{1,0:T(8,128)(2,1)} %all-gather.9.cloned.1.call-done, bf16[2048,512]{1,0:T(8,128)(2,1)S(1)} %copy-done), kind=kOutput, calls=%fused_computation.13 | convolution fusion | flops 8589934592 | bytes 27262976 | tf_op jit(solution)/shard_map/tf,th->fh/dot_general | solution.py:36
  739.3 0.0 reduce-scatter.7.cloned.1.call-start
  739.3 14.5 %fusion.7 = f32[2048,1024]{1,0:T(8,128)} fusion(bf16[2048,2048]{1,0:T(8,128)(2,1)} %get-tuple-element.10, bf16[1024,2048]{1,0:T(8,128)(2,1)} %all-gather.7.cloned.1.call-done), kind=kOutput, calls=%fused_computation.12 | convolution fusion | flops 8589934592 | bytes 20971520 | tf_op jit(solution)/shard_map/tf,hf->th/dot_general | solution.py:34
  753.9 0.0 all-reduce.3.cloned.1.call-start
  753.9 40.2 %reduce-scatter.9.cloned.1.call-done = f32[256,2048]{0,1:T(8,128)} async-done(((f32[1024,2048]{0,1:T(8,128)}), f32[256,2048]{0,1:T(8,128)}) %reduce-scatter.9.cloned.1.call-update) | async-done | bytes 2097168 | tf_op jit(solution)/shard_map/reduce_scatter | solution.py:39
  794.2 69.5 %reduce-scatter.11.cloned.1.call-done = f32[1024,512]{1,0:T(8,128)} async-done(((f32[4096,512]{1,0:T(8,128)}), f32[1024,512]{1,0:T(8,128)}) %reduce-scatter.11.cloned.1.call-update) | async-done | bytes 2097168 | tf_op jit(solution)/shard_map/reduce_scatter | solution.py:37
  863.7 99.6 %reduce-scatter.7.cloned.1.call-done = f32[2048,512]{1,0:T(8,128)} async-done(((f32[2048,1024]{1,0:T(8,128)}), f32[2048,512]{1,0:T(8,128)}) %reduce-scatter.7.cloned.1.call-update) | async-done | bytes 4194320 | tf_op jit(solution)/shard_map/reduce_scatter | solution.py:35
  963.3 3.8 convert_element_type.15
  967.1 14.7 %convolution_convert_fusion = bf16[2048,512]{1,0:T(8,128)(2,1)} fusion(bf16[2048,4096]{1,0:T(8,128)(2,1)} %all-gather.9.cloned.1.call-done, bf16[4096,512]{1,0:T(8,128)(2,1)} %all-gather.11.cloned.1.call-done), kind=kOutput, calls=%fused_computation.10 | convolution fusion | flops 8590983168 | bytes 23068672 | tf_op jit(solution)/shard_map/tf,fh->th/dot_general | solution.py:30
  981.8 88.0 %all-reduce.3.cloned.1.call-done = (f32[256,2048]{0,1:T(8,128)}, f32[1024,512]{1,0:T(8,128)}) async-done(((f32[256,2048]{0,1:T(8,128)}, f32[1024,512]{1,0:T(8,128)}), (f32[256,2048]{0,1:T(8,128)}, f32[1024,512]{1,0:T(8,128)})) %all-reduce.3.cloned.1.call-update) | async-done | bytes 4194320 | tf_op jit(solution)/shard_map/psum | solution.py:39
  1069.7 2.9 copy.8
  1072.6 3.1 copy.11
  (8 shorter events, 0.1 us)
Async XLA Ops:
  7.2 37.6 %copy-start = (bf16[2048,512]{1,0:T(8,128)(2,1)S(1)}, bf16[2048,512]{1,0:T(8,128)(2,1)}, u32[]{:S(2)}) copy-start(bf16[2048,512]{1,0:T(8,128)(2,1)} %param.7) | copy-start | bytes 6291460
  7.2 37.6 %all-gather.11.cloned.1.call-start = ((), (), s32[]{:S(2)}) async-start(), calls=%async_computation.7 | async-start | bytes 5242880 | tf_op jit(solution)/shard_map/all_gather | solution.py:26
  7.9 93.5 %all-gather.5.cloned.1.call-start = ((), (), s32[]{:S(2)}) async-start(), calls=%async_computation.4 | async-start | bytes 6291456 | tf_op jit(solution)/shard_map/all_gather | solution.py:24
  8.7 126.8 %all-gather.7.cloned.1.call-start = ((), (), s32[]{:S(2)}) async-start(), calls=%async_computation.5 | async-start | bytes 5242880 | tf_op jit(solution)/shard_map/all_gather | solution.py:25
  9.4 495.2 %reduce-scatter.5.cloned.1.call-start = ((), (), s32[]{:S(2)}) async-start(), calls=%async_computation.8 | async-start | bytes 50331648 | tf_op jit(solution)/shard_map/reduce_scatter | solution.py:32
  61.5 663.2 %all-gather.9.cloned.1.call-start = ((), (), s32[]{:S(2)}) async-start(), calls=%async_computation.6 | async-start | bytes 25165824 | tf_op jit(solution)/shard_map/all_gather | solution.py:29
  527.0 267.1 %reduce-scatter.9.cloned.1.call-start = ((), (), s32[]{:S(2)}) async-start(), calls=%async_computation.10 | async-start | bytes 10485760 | tf_op jit(solution)/shard_map/reduce_scatter | solution.py:39
  541.7 322.0 %reduce-scatter.11.cloned.1.call-start = ((), (), s32[]{:S(2)}) async-start(), calls=%async_computation.11 | async-start | bytes 10485760 | tf_op jit(solution)/shard_map/reduce_scatter | solution.py:37
  739.3 224.0 %reduce-scatter.7.cloned.1.call-start = ((), (), s32[]{:S(2)}) async-start(), calls=%async_computation.9 | async-start | bytes 12582912 | tf_op jit(solution)/shard_map/reduce_scatter | solution.py:35
  753.9 315.9 %all-reduce.3.cloned.1.call-start = ((), (), s32[]{:S(2)}) async-start(), calls=%async_computation.12 | async-start | bytes 8388608 | tf_op jit(solution)/shard_map/psum | solution.py:39
  967.1 108.6 %copy-start.1 = (bf16[2048,512]{1,0:T(8,128)(2,1)S(1)}, bf16[2048,512]{1,0:T(8,128)(2,1)}, u32[]{:S(2)}) copy-start(bf16[2048,512]{1,0:T(8,128)(2,1)} %param.7) | copy-start | bytes 6291460
Sparse Core Ops, SparseCore 0:
  9.5 35.2 all-gather.10
  46.3 55.0 all-gather.4
  103.0 32.3 all-gather.6
  137.6 366.9 reduce-scatter.4
  527.1 197.6 all-gather.8
  727.2 66.9 reduce-scatter.8
  796.7 66.9 reduce-scatter.10
  865.9 97.3 reduce-scatter.6
  965.8 103.8 all-reduce.2
where the time goes:
time: 1080 us
  waiting for transfers between devices  961 us (89%)
  matrix products  97.3 us (9%)
  between operations  13.9 us (1%)
    reduce_scatter x1, waiting for transfers between devices, grid_block(): lax.psum_scatter(act_part, 'col', scatter_dimension=1, tiled=True)  369 us
    all_gather x1, waiting for transfers between devices, grid_block(): act_rows = lax.all_gather(hidden_act, 'col', axis=1, tiled=True)  183 us
    reduce_scatter x1, waiting for transfers between devices, grid_block(): lax.psum_scatter(tok_part, 'col', scatter_dimension=1, tiled=True)  99.6 us
    psum x1, waiting for transfers between devices, grid_block(): lax.psum(lax.psum_scatter(up_part, 'row', scatter_dimension=0, tiled=True...  88 us
    reduce_scatter x1, waiting for transfers between devices, grid_block(): lax.psum_scatter(down_part, 'row', scatter_dimension=0, tiled=True)  69.5 us
    reduce_scatter x1, waiting for transfers between devices, grid_block(): lax.psum_scatter(up_part, 'row', scatter_dimension=0, tiled=True)  40.2 us
    all_gather x1, waiting for transfers between devices, grid_block(): tok_rows = lax.all_gather(tok_blk, 'col', axis=1, tiled=True)  39.9 us
    all_gather x1, waiting for transfers between devices, grid_block(): down_cols = lax.all_gather(down_blk, 'row', axis=0, tiled=True)  35.4 us
  transfers between devices with their start and end apart: 9, of which 9 were waited for; matrix products, arithmetic and copies ran while one was open for 7% of the time, Pallas kernels for 0%

commit v1 on v0

v1 whole, which is shorter than its diff:
```python
import math
import jax
import jax.numpy as jnp
from jax import lax
from jax.experimental import pallas as pl
from jax.experimental.pallas import tpu as pltpu
from jax.sharding import PartitionSpec as P

INV_ROOT_TWO = 1.0 / math.sqrt(2.0)
INV_ROOT_TAU = 1.0 / math.sqrt(2.0 * math.pi)
MESH = pl.DeviceIdType.MESH
BF16, F32 = jnp.bfloat16, jnp.float32

TOK, HID, FC, NCH = 2048, 1024, 256, 8
HALF, TILE = 512, 512
Z2, X1, X2, Y2, Y1, Z1, ZO, C1, CP, YO = 0, 8, 16, 20, 24, 28, 32, 36, 40, 42
WY1, WX1, WP, WF1, WY2, WX2, WF2, TY, TP, TF, NSEM = 44, 52, 60, 64, 68, 72, 76, 80, 82, 84, 86


def dot(a, b, ca, cb):
    return lax.dot_general(a, b, (((ca,), (cb,)), ((), ())), preferred_element_type=F32)


def kernel(x_in, g_in, up_in, down_in, y_out, dx_out, d1_out, d2_out, yl, dl, w1b, w2b,
           xs, gs, yacc, dxacc, d1, d2, zr2, xr1, xr2, yr2, yr1, zr1, w1s, w2s, stage,
           send, recv, loc, wsem, isem):
    z, y, r = lax.axis_index("depth"), lax.axis_index("col"), lax.axis_index("row")
    x, c = r // 2, r % 2
    dev_c, dev_x = (z, y, r + 1 - 2 * c), (z, y, (1 - x) * 2 + c)
    dev_y, dev_z = (z, 1 - y, r), (1 - z, y, r)
    dev_xc, dev_yc = (z, y, (1 - x) * 2 + 1 - c), (z, 1 - y, r + 1 - 2 * c)
    zrow = pl.ds(pl.multiple_of(z * 128, 128), 128)
    zoth = pl.ds(pl.multiple_of((1 - z) * 128, 128), 128)
    lo, hi = pl.ds(0, HALF), pl.ds(HALF, HALF)
    mine, theirs = pl.ds(0, TOK // 2), pl.ds(TOK // 2, TOK // 2)
    tok_rows = pl.ds(pl.multiple_of(y * (TOK // 2), TOK // 2), TOK // 2)
    oth_rows = pl.ds(pl.multiple_of((1 - y) * (TOK // 2), TOK // 2), TOK // 2)

    def rc2(ks, kr, src, dst, dev):
        return pltpu.make_async_remote_copy(src_ref=src, dst_ref=dst, send_sem=send.at[ks], recv_sem=recv.at[kr],
                                            device_id=dev, device_id_type=MESH)

    def rc(k, src, dst, dev):
        return rc2(k, k, src, dst, dev)

    barrier = pltpu.get_barrier_semaphore()
    for dev in (dev_c, dev_x, dev_y, dev_z, dev_xc, dev_yc):
        pl.semaphore_signal(barrier, inc=1, device_id=dev, device_id_type=MESH)
    pl.semaphore_wait(barrier, 6)

    def chunk(q):
        return pl.ds(pl.multiple_of(q * FC, FC), FC)

    def up_cols(core, s):
        return pl.ds(pl.multiple_of(core * HID + s * FC, FC), FC)

    def t_wy1(s, core, sender):
        dev = (z, 1 - y, x * 2 + core)
        return rc2(WY1 + 2 * s + core, WY1 + 2 * s + sender, up_in.at[:, up_cols(core, s)],
                   w1b.at[y, chunk(c), chunk(s)], dev)

    def t_wx1(s, core, sender):
        dev = (z, y, (1 - x) * 2 + core)
        return rc2(WX1 + 2 * s + core, WX1 + 2 * s + sender, up_in.at[:, up_cols(core, s)],
                   w1b.at[y, chunk(2 + c), chunk(s)], dev)

    def t_wp(s):
        return rc(WP + s, up_in.at[:, up_cols(1 - c, s)], w1b.at[y, chunk(c), chunk(s)], dev_c)

    def t_wf1(s):
        return rc(WF1 + s, w1b.at[1 - y, lo, chunk(s)], w1b.at[1 - y, hi, chunk(s)], dev_x)

    def t_wy2(s):
        return rc(WY2 + s, down_in.at[chunk(s), :], w2b.at[x, chunk(s), hi], dev_y)

    def t_wx2(s):
        return rc(WX2 + s, down_in.at[chunk(s), :], w2b.at[x, chunk(s), lo], dev_x)

    def t_wf2(s):
        return rc(WF2 + s, w2b.at[x, chunk(s), hi], w2b.at[x, chunk(s), hi], dev_x)

    def send_wy(s):
        for core in (0, 1):
            t_wy1(s, core, c).start()
        t_wy2(s).start()

    def send_wx(s):
        for core in (0, 1):
            t_wx1(s, core, c).start()
        t_wx2(s).start()
        t_wp(s).start()

    def forward_w(s):
        for core in (0, 1):
            t_wy1(s, core, core).wait_recv()
        t_wy2(s).wait_recv()
        t_wf1(s).start()
        t_wf2(s).start()

    def arrive_w(s):
        for core in (0, 1):
            t_wx1(s, core, core).wait_recv()
        t_wx2(s).wait_recv()
        t_wp(s).wait_recv()
        t_wf1(s).wait_recv()
        t_wf2(s).wait_recv()

    eq_off = pl.multiple_of(jnp.where(x == y, 0, HALF), HALF)
    ne_off = pl.multiple_of(jnp.where(x == y, HALF, 0), HALF)
    own_cols = (pl.ds(eq_off, HALF), lo)
    far_cols = (pl.ds(ne_off, HALF), hi)

    def t_ty(i):
        return rc(TY + i, (x_in, g_in)[i].at[oth_rows, :], (xs, gs)[i].at[mine, (own_cols[0], hi)[i]], dev_y)

    def t_tp(i):
        return rc(TP + i, (x_in, g_in)[i].at[tok_rows, :], (xs, gs)[i].at[theirs, own_cols[i]], dev_c)

    def t_tf(i):
        return rc(TF + i, (xs, gs)[i].at[mine, far_cols[i]], (xs, gs)[i].at[theirs, far_cols[i]], dev_c)

    def l_t(i):
        return pltpu.make_async_copy((x_in, g_in)[i].at[tok_rows, :], (xs, gs)[i].at[mine, own_cols[i]], isem.at[i])

    send_wy(0)
    send_wx(0)
    for i in (0, 1):
        t_ty(i).start()
        l_t(i).start()
        t_tp(i).start()
    send_wx(1)
    for s in (1, 2, 3):
        send_wy(s)

    def load_w(j, slot, start):
        s, b = j // 2, j % 2

        def go(src, dst, k):
            cp = pltpu.make_async_copy(src, dst, wsem.at[slot, k])
            cp.start() if start else cp.wait()
        v1, v2 = w1s.at[slot], w2s.at[slot]
        if start:
            @pl.when(b == y)
            def _():
                go(up_in.at[:, up_cols(c, s)], v1.at[chunk(c), :], 0)

            @pl.when(b != y)
            def _():
                go(w1b.at[b, chunk(c), chunk(s)], v1.at[chunk(c), :], 0)

            @pl.when(b == x)
            def _():
                go(down_in.at[chunk(s), :], v2.at[:, lo], 3)

            @pl.when(b != x)
            def _():
                go(w2b.at[b, chunk(s), lo], v2.at[:, lo], 3)
        else:
            go(up_in.at[:, up_cols(c, s)], v1.at[chunk(c), :], 0)
            go(down_in.at[chunk(s), :], v2.at[:, lo], 3)
        go(w1b.at[b, chunk(1 - c), chunk(s)], v1.at[chunk(1 - c), :], 1)
        go(w1b.at[b, hi, chunk(s)], v1.at[hi, :], 2)
        go(w2b.at[b, chunk(s), hi], v2.at[:, hi], 4)

    def zero(i, _):
        rows = pl.ds(pl.multiple_of(i * 64, 64), 64)
        yacc[rows, :] = jnp.zeros((64, HID), F32)
        dxacc[rows, :] = jnp.zeros((64, HID), F32)
        return 0
    lax.fori_loop(0, TOK // 64, zero, 0)
    forward_w(0)
    send_wx(2)
    send_wx(3)
    arrive_w(0)
    load_w(0, 0, True)
    for i in (0, 1):
        t_ty(i).wait_recv()
        t_tf(i).start()
        l_t(i).wait()
        t_tp(i).wait_recv()
    for i in (0, 1):
        t_tf(i).wait_recv()

    def t_z2(j):
        return rc(Z2 + j, d2.at[j, zoth, :], zr2.at[j], dev_z)

    def t_x1(j):
        return rc(X1 + j, d1.at[j, :, hi], xr1.at[j], dev_x)

    def t_x2(s):
        return rc(X2 + s, d2.at[2 * s + 1 - x, zrow, :], xr2.at[s], dev_x)

    def t_y1(s):
        return rc(Y1 + s, d1.at[2 * s + 1 - y, :, lo], yr1.at[s], dev_y)

    def t_y2(s):
        return rc(Y2 + s, d2.at[2 * s + x, zrow, hi], yr2.at[s], dev_y)

    def t_z1(s):
        return rc(Z1 + s, d1.at[2 * s + y, :, lo], zr1.at[s], dev_z)

    def o2_rows(s):
        return d2_out.at[pl.ds(pl.multiple_of(s * FC + z * 128, 128), 128), :]

    def o1_rows(s):
        return d1_out.at[pl.ds(pl.multiple_of(c * HID + s * FC, FC), FC), :]

    def cols_c(q):
        return pl.ds(pl.multiple_of(q * 256, 256), 256)

    def t_zo(s):
        return rc(ZO + s, yr2.at[s], o2_rows(s), dev_z)

    def t_zo_in(s):
        return rc(ZO + s, yr2.at[s], d2_out.at[pl.ds(pl.multiple_of(s * FC + (1 - z) * 128, 128), 128), :], dev_z)

    def l_o2(s):
        return pltpu.make_async_copy(yr2.at[s], o2_rows(s), loc.at[s])

    def t_c1(s):
        return rc(C1 + s, zr1.at[s, :, cols_c(1 - c)], o1_rows(s), dev_c)

    def l_o1(s):
        return pltpu.make_async_copy(zr1.at[s, :, cols_c(c)], o1_rows(s), loc.at[4 + s])

    def t_cp(i):
        return rc(CP + i, (yacc, dxacc)[i].at[theirs, :], (yl, dl)[i], dev_c)

    def compute(j):
        slot = j % 2

        load_w(j, slot, False)
        w1, w2 = w1s.at[slot], w2s.at[slot]

        def tile(t, _):
            rows = pl.ds(pl.multiple_of(t * TILE, TILE), TILE)

            @pl.when(jnp.logical_and(t == TOK // TILE - 1, j + 1 < NCH))
            def _():
                @pl.when(slot == 1)
                def _():
                    arrive_w((j + 1) // 2)
                load_w(j + 1, 1 - slot, True)
            xt, gt = xs[rows, :], gs[rows, :]
            u = dot(xt, w1[...], 1, 0)
            da = dot(gt, w2[...], 1, 1)
            cdf = 0.5 * (1.0 + lax.erf(u * INV_ROOT_TWO))
            act = (u * cdf).astype(BF16)
            du = (da * (cdf + u * jnp.exp(-0.5 * u * u) * INV_ROOT_TAU)).astype(BF16)
            yacc[rows, :] += dot(act, w2[...], 1, 0)
            dxacc[rows, :] += dot(du, w1[...], 1, 1)
            p2, p1 = dot(act, gt, 0, 0), dot(du, xt, 0, 0)

            @pl.when(t == 0)
            def _():
                d2[j] = p2
                d1[j] = p1

            @pl.when(t > 0)
            def _():
                d2[j] += p2
                d1[j] += p1
            return 0
        lax.fori_loop(0, TOK // TILE, tile, 0)
        t_z2(j).start()
        t_x1(j).start()

    def stage_b(j):
        t_z2(j).wait_recv()
        d2[j, zrow, :] += zr2[j]
        t_x1(j).wait_recv()
        d1[j, :, :HALF] += xr1[j]

    def stage_c(s):
        t_x2(s).start()
        t_y1(s).start()

    def stage_d(s):
        t_x2(s).wait_recv()
        d2[2 * s + x, zrow, :] += xr2[s]
        t_y2(s).start()
        t_y1(s).wait_recv()
        d1[2 * s + y, :, :HALF] += yr1[s]
        t_z1(s).start()

    def stage_e(s):
        t_y2(s).wait_recv()
        yr2[s] += d2[2 * s + x, zrow, :HALF]
        t_zo(s).start()
        l_o2(s).start()
        t_z1(s).wait_recv()
        zr1[s] += d1[2 * s + y, :, :HALF]
        t_c1(s).start()
        l_o1(s).start()

    def step(j, _):
        @pl.when(j < NCH)
        def _():
            compute(j)

        @pl.when(j < 3)
        def _():
            forward_w(j + 1)

        @pl.when(j == NCH - 1)
        def _():
            t_cp(0).start()
            t_cp(1).start()

        @pl.when(j >= 1)
        def _():
            stage_b(j - 1)
        even = j % 2 == 0

        @pl.when(jnp.logical_and(even, j >= 2))
        def _():
            stage_c(j // 2 - 1)

        @pl.when(jnp.logical_and(jnp.logical_not(even), j >= 3))
        def _():
            stage_d((j - 3) // 2)

        @pl.when(jnp.logical_and(even, j >= 4))
        def _():
            stage_e(j // 2 - 2)
        return 0
    lax.fori_loop(0, NCH + 1, step, 0)

    def fin_cols(i, own):
        return (hi, far_cols[0], lo, own_cols[0])[2 * own + i]

    def t_yo(i, rows):
        return rc(YO + i, (xs, gs)[i].at[mine, fin_cols(i, False)], (y_out, dx_out)[i].at[rows, :], dev_y)

    def l_yo(i):
        return pltpu.make_async_copy((xs, gs)[i].at[mine, fin_cols(i, True)], (y_out, dx_out)[i].at[tok_rows, :],
                                     loc.at[8 + i])

    def finish(i):
        t_cp(i).wait_recv()
        acc, part, dst = (yacc, dxacc)[i], (yl, dl)[i], (xs, gs)[i]

        def fetch(q, slot):
            return pltpu.make_async_copy(part.at[pl.ds(pl.multiple_of(q * 128, 128), 128), :], stage.at[slot],
                                         isem.at[slot])
        fetch(0, 0).start()

        def piece(q, _):
            slot = q % 2

            @pl.when(q < 7)
            def _():
                fetch(q + 1, 1 - slot).start()
            fetch(q, slot).wait()
            rows = pl.ds(pl.multiple_of(q * 128, 128), 128)
            dst[rows, :] = (acc[rows, :] + stage[slot]).astype(BF16)
            return 0
        lax.fori_loop(0, 8, piece, 0)
        t_yo(i, tok_rows).start()
        l_yo(i).start()

    for i in (0, 1):
        t_tf(i).wait_send()
    finish(0)
    stage_d(3)
    finish(1)
    stage_e(3)

    def drain8(j, _):
        t_z2(j).wait_send()
        t_x1(j).wait_send()
        return 0
    lax.fori_loop(0, NCH, drain8, 0)

    def drain4(s, _):
        for t in (t_x2, t_y1, t_y2, t_z1, t_zo, t_c1):
            t(s).wait_send()
        t_zo_in(s).wait_recv()
        t_c1(s).wait_recv()
        l_o2(s).wait()
        l_o1(s).wait()
        return 0
    lax.fori_loop(0, NCH // 2, drain4, 0)

    def drain_w(s, _):
        for core in (0, 1):
            t_wy1(s, core, c).wait_send()
            t_wx1(s, core, c).wait_send()
        for t in (t_wp, t_wf1, t_wy2, t_wx2, t_wf2):
            t(s).wait_send()
        return 0
    lax.fori_loop(0, NCH // 2, drain_w, 0)
    for i in (0, 1):
        for t in (t_ty, t_tp, t_cp):
            t(i).wait_send()
        t_yo(i, tok_rows).wait_send()
        t_yo(i, oth_rows).wait_recv()
        l_yo(i).wait()


def fused(tok, grad, up, down):
    any_spec = pl.BlockSpec(memory_space=pl.ANY)
    vm = pltpu.VMEM
    shape = jax.ShapeDtypeStruct
    return pl.pallas_call(
        kernel,
        name="mlp_block",
        out_shape=(shape((TOK, HALF), BF16), shape((TOK, HALF), BF16), shape((2048, 256), F32), shape((1024, HALF), F32),
                   shape((TOK // 2, HID), F32), shape((TOK // 2, HID), F32),
                   shape((2, HID, HID), BF16), shape((2, HID, HID), BF16)),
        in_specs=[any_spec] * 4,
        out_specs=[any_spec] * 8,
        scratch_shapes=[
            vm((TOK, HID), BF16), vm((TOK, HID), BF16), vm((TOK, HID), F32), vm((TOK, HID), F32),
            vm((NCH, FC, HID), F32), vm((NCH, FC, HID), F32),
            vm((NCH, 128, HID), F32), vm((NCH, FC, HALF), F32),
            vm((4, 128, HID), F32), vm((4, 128, HALF), F32), vm((4, FC, HALF), F32), vm((4, FC, HALF), F32),
            vm((2, HID, FC), BF16), vm((2, FC, HID), BF16), vm((2, 128, HID), F32),
            pltpu.SemaphoreType.DMA((NSEM,)), pltpu.SemaphoreType.DMA((NSEM,)), pltpu.SemaphoreType.DMA((10,)),
            pltpu.SemaphoreType.DMA((2, 5)), pltpu.SemaphoreType.DMA((2,)),
        ],
        compiler_params=pltpu.CompilerParams(collective_id=0, has_side_effects=True, vmem_limit_bytes=67_043_328),
    )(tok, grad, up, down)


def solution(mesh):
    act_spec = P(("depth", "row"), "col")
    wgt_spec = P("row", "col")

    def block(tok, up, down, grad):
        out = fused(tok, grad, up, down)
        return out[0], out[1], out[2].T, out[3]

    return jax.shard_map(block, mesh=mesh, in_specs=(act_spec, wgt_spec, wgt_spec, act_spec),
                         out_specs=(act_spec, act_spec, wgt_spec, wgt_spec), check_vma=False)
```

time: 1080 us -> 318 us (0.29)
  waiting for transfers between devices: 961 us -> 0 us
  Pallas kernels: 0 us -> 308 us
  matrix products: 97.3 us -> 0 us
  between operations: 13.9 us -> 0.65 us
    reduce_scatter x4 -> x0, waiting for transfers between devices: 579 us -> none  [the longest x1 369 us: grid_block(): lax.psum_scatter(act_part, 'col', scatter_dimension=1, tiled=True)]
    pallas_call x0 -> x1, Pallas kernels: none -> 308 us  [fused(): pl.pallas_call(kernel, name='mlp_block', out_shape=(shape((TOK, HALF), BF...]
    all_gather x4 -> x0, waiting for transfers between devices: 292 us -> none  [the longest x1 183 us: grid_block(): act_rows = lax.all_gather(hidden_act, 'col', axis=1, tiled=True)]
    dot_general x6 -> x0, matrix products: 97.3 us -> none  [the longest x1 22.4 us: grid_block(): jnp.einsum('th,hf->tf', tok_rows, up_cols, preferred_element_type=jnp.flo...]
    psum x1 -> x0, waiting for transfers between devices: 88 us -> none  [grid_block(): lax.psum(lax.psum_scatter(up_part, 'row', scatter_dimension=0, tiled=True...]
  transfers between devices with their start and end apart: 9 -> 0, of which waited for: 9 -> 0; matrix products, arithmetic and copies ran while one was open for 7% -> 0% of each run, Pallas kernels for 0% -> 0%
where the time goes in v1:
time: 318 us; the launch traced here: 317 us
  Pallas kernels  308 us (97%)
  local copies, waits for them, and re-layouts  9.05 us (3%)
    pallas_call x1, Pallas kernels, fused(): pl.pallas_call(kernel, name='mlp_block', out_shape=(shape((TOK, HALF), BF...  308 us
    unnamed x10, local copies, waits for them, and re-layouts  9.05 us

profile of v1, /device:TPU:0, one launch (start us, length us, event | category | flops | bytes accessed | tf_op | source)
XLA Modules:
  0.0 317.3 jit_solution(4654429035651548931)
XLA Ops:
  0.6 307.6 %mlp_block.1 = (bf16[2048,512]{1,0:T(8,128)(2,1)}, bf16[2048,512]{1,0:T(8,128)(2,1)}, f32[2048,256]{1,0:T(8,128)}, f32[1024,512]{1,0:T(8,128)}, f32[1024,1024]{1...) custom-call(bf16[2048,512]{1,0:T(8,128)(2,1)} %x_in.1, ...), custom_call_target="tpu_custom_call" | custom-call | tf_op jit(solution)/shard_map/mlp_block/pallas_call | solution.py:405
  308.2 0.0 copy-start.2
  308.2 3.0 copy.8
  311.2 0.0 copy-done.2
  311.2 0.0 copy-start.1
  311.2 1.3 copy.12
  312.6 1.0 copy-done.1
  313.6 0.0 copy-start
  313.6 1.3 copy.13
  314.9 1.0 copy-done
  315.9 1.3 copy.14
Async XLA Ops:
  308.2 3.0 copy-start.2
  311.2 2.3 copy-start.1
  313.6 2.3 copy-start

commit v2 on v0

v2 whole, which is shorter than its diff:
```python
import math
import jax
import jax.numpy as jnp
from jax import lax
from jax.experimental import pallas as pl
from jax.experimental.pallas import tpu as pltpu
from jax.sharding import PartitionSpec as P

INV_ROOT_TWO = 1.0 / math.sqrt(2.0)
INV_ROOT_TAU = 1.0 / math.sqrt(2.0 * math.pi)
MESH = pl.DeviceIdType.MESH
BF16, F32 = jnp.bfloat16, jnp.float32

TOK, HID, FC, NCH = 2048, 1024, 256, 8
HALF, TILE, ROWS = 512, 512, 128
NT = TOK // TILE
FIRST = ("wy0", "t0", "wy1", "t1", "wy2", "wy3", "wxo0", "wxo1", "wxo2", "wxo3",)
ORDERS = {1: ("ZCB", "CZB", "CBZ", "CZB"),
          2: ("CZB", "CBZ", "CBZ", "ZBC")}
PLAN = {
    0: ("fw0", "fzx0", "fzx1", "fzx2", "fzx3", "ft0", "fz0", "fw1", "fz1", "lw0", "lw1",),
    2: ("ft1",),
    4: ("fw2", "lw2", "s1000", "s2000",),
    6: ("fw3",),
    8: ("fz2", "lw3", "s1001", "s2001",),
    10: ("fz3", "b1000",),
    11: ("b2000",),
    12: ("s1100", "s2100",),
    15: ("lw4", "b2001", "s201",),
    16: ("lw5", "s1101", "s2101",),
    18: ("b1100",),
    19: ("b1001", "s101",),
    20: ("s1200", "s2200", "b2100",),
    22: ("b1101", "s111",),
    23: ("lw6",),
    24: ("lw7", "s1201", "s2201", "b2101", "s211",),
    26: ("b101", "s102",),
    28: ("s1300", "s2300", "b201", "b2200", "s202",),
    31: ("b1200",),
    32: ("cp", "s1301", "s2301", "b111", "s112", "b2201", "s221", "b102", "b1201", "s121", "b2300", "fin0",
        "b112", "b211", "s212", "fin1", "b2301", "b121", "s231", "s122", "b1300", "b202", "b212", "b1301",
        "s131", "b122", "b221", "s222", "b231", "s232", "b131", "s132", "b232", "b132", "b222",),
}

def dot(a, b, ca, cb):
    return lax.dot_general(a, b, (((ca,), (cb,)), ((), ())), preferred_element_type=F32)


def hop_shapes(order):
    nb, rows, cols, shapes = 2, FC, HID, []
    for h, kind in enumerate(order):
        if kind == "B":
            nb = 1
        elif kind == "C":
            cols = HALF
        elif h < 2:
            rows = ROWS
        shapes.append((nb, rows, cols))
    return shapes


def kernel(x_in, g_in, up_in, down_in, y_out, dx_out, d1_out, d2_out, yl, dl, w1b, w2b,
           xs, gs, yacc, dxacc, d1, d2, w1s, w2s, send, recv, loc, wsem, isem, *land):
    z, y, r = lax.axis_index("depth"), lax.axis_index("col"), lax.axis_index("row")
    x, c = r // 2, r % 2
    r_x = (1 - x) * 2 + c
    r_c = r + 1 - 2 * c
    dev_c, dev_x, dev_xc = (z, y, r_c), (z, y, r_x), (z, y, (1 - x) * 2 + 1 - c)
    dev_y, dev_yc, dev_z, dev_zc = (z, 1 - y, r), (z, 1 - y, r_c), (1 - z, y, r), (1 - z, y, r_c)
    everything, lo, hi = slice(None), pl.ds(0, HALF), pl.ds(HALF, HALF)
    zrow = pl.ds(pl.multiple_of(z * ROWS, ROWS), ROWS)
    zoth = pl.ds(pl.multiple_of((1 - z) * ROWS, ROWS), ROWS)
    slots = {}

    def slot_of(name):
        return slots.setdefault(name, len(slots))

    def rc(name, src, dst, dev, arrives=None):
        return pltpu.make_async_remote_copy(
            src_ref=src, dst_ref=dst, send_sem=send.at[slot_of(name)],
            recv_sem=recv.at[slot_of(name if arrives is None else arrives)], device_id=dev, device_id_type=MESH)

    def go(*copies):
        for cp in copies:
            cp.start()

    def got(*copies):
        for cp in copies:
            cp.wait_recv()

    barrier = pltpu.get_barrier_semaphore()
    for dev in (dev_c, dev_x, dev_xc, dev_y, dev_yc, dev_z, dev_zc):
        pl.semaphore_signal(barrier, inc=1, device_id=dev, device_id_type=MESH)
    pl.semaphore_wait(barrier, 7)

    def chunk(q):
        return pl.ds(pl.multiple_of(q * FC, FC), FC)

    def up_cols(core, s):
        return pl.ds(pl.multiple_of(core * HID + s * FC, FC), FC)

    def part(xh, core, zi):
        return pl.ds(pl.multiple_of(xh * HALF + core * FC + zi * ROWS, ROWS), ROWS)

    def down_rows(s):
        return pl.ds(pl.multiple_of(s * FC + z * ROWS, ROWS), ROWS)

    def by_core(name, s, core, src, dst, dev):
        base = slot_of(f"{name}{s}0")
        slot_of(f"{name}{s}1")
        return pltpu.make_async_remote_copy(src_ref=src, dst_ref=dst, send_sem=send.at[base + core],
                                            recv_sem=recv.at[base + c], device_id=dev, device_id_type=MESH)

    def by_core_in(name, s, core, like):
        base = slot_of(f"{name}{s}0")
        slot_of(f"{name}{s}1")
        return pltpu.make_async_remote_copy(src_ref=like, dst_ref=like, send_sem=send.at[base + core],
                                            recv_sem=recv.at[base + core], device_id=dev_c, device_id_type=MESH)

    def wy(s):
        two = [by_core("wy", s, q, up_in.at[zrow, up_cols(q, s)], w1b.at[y, part(0, c, z), chunk(s)], (z, 1 - y, x * 2 + q))
               for q in (0, 1)]
        return two + [wy_down(s)]

    def wy_down(s):
        return rc(f"wY{s}", down_in.at[down_rows(s), :], w2b.at[x, down_rows(s), hi], dev_y)

    def wy_in(s):
        return [by_core_in("wy", s, q, w1b.at[1 - y, part(0, q, z), chunk(s)]) for q in (0, 1)] + [wy_down(s)]

    def wx(s):
        two = [by_core("wx", s, q, up_in.at[zrow, up_cols(q, s)], w1b.at[y, part(1, c, z), chunk(s)],
                       (z, y, (1 - x) * 2 + q)) for q in (0, 1)]
        return two + [wx_down(s)]

    def wx_down(s):
        return rc(f"wX{s}", down_in.at[down_rows(s), :], w2b.at[x, down_rows(s), lo], dev_x)

    def wx_in(s):
        return [by_core_in("wx", s, q, w1b.at[y, part(1, q, z), chunk(s)]) for q in (0, 1)] + [wx_down(s)]

    def wp(s):
        return [rc(f"wp{s}", up_in.at[:, up_cols(1 - c, s)], w1b.at[y, chunk(c), chunk(s)], dev_c)]

    def wf(s):
        two = [rc(f"wf{s}{q}", w1b.at[1 - y, part(0, q, z), chunk(s)], w1b.at[1 - y, part(1, q, z), chunk(s)], dev_x)
               for q in (0, 1)]
        both = w2b.at[x, down_rows(s), hi]
        return two + [rc(f"wF{s}", both, both, dev_x)]

    def same_z(name, ref):
        return rc(name, ref, ref, dev_z)

    def wzx(s):
        return [same_z(f"wzx{s}{q}", w1b.at[y, part(1, q, z), chunk(s)]) for q in (0, 1)] + [
            same_z(f"wzX{s}", w2b.at[1 - x, down_rows(s), lo])]

    def wz(s):
        return [same_z(f"wz{s}{h}{q}", w1b.at[1 - y, part(h, q, z), chunk(s)]) for h in (0, 1) for q in (0, 1)] + [
            same_z(f"wZ{s}{i}", w2b.at[(x, 1 - x)[i], down_rows(s), hi]) for i in (0, 1)]

    def load_w(j, slot, start):
        s, b = j // 2, j % 2

        def cp(src, dst, k):
            copy = pltpu.make_async_copy(src, dst, wsem.at[slot, k])
            copy.start() if start else copy.wait()
        v1, v2 = w1s.at[slot], w2s.at[slot]
        if start:
            @pl.when(b == y)
            def _():
                cp(up_in.at[:, up_cols(c, s)], v1.at[chunk(c), :], 0)

            @pl.when(b != y)
            def _():
                cp(w1b.at[b, chunk(c), chunk(s)], v1.at[chunk(c), :], 0)

            @pl.when(b == x)
            def _():
                cp(down_in.at[chunk(s), :], v2.at[:, lo], 3)

            @pl.when(b != x)
            def _():
                cp(w2b.at[b, chunk(s), lo], v2.at[:, lo], 3)
        else:
            cp(up_in.at[:, up_cols(c, s)], v1.at[chunk(c), :], 0)
            cp(down_in.at[chunk(s), :], v2.at[:, lo], 3)
        cp(w1b.at[b, chunk(1 - c), chunk(s)], v1.at[chunk(1 - c), :], 1)
        cp(w1b.at[b, hi, chunk(s)], v1.at[hi, :], 2)
        cp(w2b.at[b, chunk(s), hi], v2.at[:, hi], 4)

    own_cols = (pl.ds(pl.multiple_of(jnp.where(x == y, 0, HALF), HALF), HALF), lo)
    far_cols = (pl.ds(pl.multiple_of(jnp.where(x == y, HALF, 0), HALF), HALF), hi)
    ins, tok = (x_in, g_in), (xs, gs)

    def tok_at(base, i):
        return pl.ds(pl.multiple_of(base * (TOK // 2) + i * TILE, TILE), TILE)

    def ty(i):
        return [rc(f"ty{i}{k}", ins[k].at[tok_at(1 - y, i), :], tok[k].at[tok_at(0, i), (own_cols[0], hi)[k]], dev_y)
                for k in (0, 1)]

    def tp(i):
        return [rc(f"tp{i}{k}", ins[k].at[tok_at(y, i), :], tok[k].at[tok_at(1, i), own_cols[k]], dev_c) for k in (0, 1)]

    def tf(i):
        return [rc(f"tf{i}{k}", tok[k].at[tok_at(0, i), far_cols[k]], tok[k].at[tok_at(1, i), far_cols[k]], dev_c)
                for k in (0, 1)]

    def tl(i):
        return [pltpu.make_async_copy(ins[k].at[tok_at(y, i), :], tok[k].at[tok_at(0, i), own_cols[k]],
                                      isem.at[2 * i + k]) for k in (0, 1)]

    parts = {1: d1, 2: d2}
    buf = {(m, s, h): land[(m - 1) * 12 + s * 3 + h] for m in (1, 2) for s in range(4) for h in range(3)}
    keep_block = {1: y, 2: x}
    dev_of = {(1, "C"): dev_x, (1, "B"): dev_y, (1, "Z"): dev_z, (2, "C"): dev_y, (2, "B"): dev_x, (2, "Z"): dev_z}

    def live(m, s, h):
        blocks, rows, cols = [2 * s, 2 * s + 1], everything, everything
        for kind in ORDERS[m][s][:h]:
            if kind == "B":
                blocks = [2 * s + keep_block[m]]
            elif kind == "C":
                cols = lo
            else:
                rows = zrow
        return blocks, rows, cols

    def hop(m, s, h, only=None):
        kind = ORDERS[m][s][h]
        blocks, rows, cols = live(m, s, h)
        d, b, dev = parts[m], buf[m, s, h], dev_of[m, kind]
        if kind == "B":
            ends = [(d.at[2 * s + 1 - keep_block[m], rows, cols], (2 * s + keep_block[m], rows, cols))]
        elif kind == "C":
            ends = [(d.at[q, rows, hi], (q, rows, lo)) for q in blocks]
        elif h < 2:
            ends = [(d.at[q, zoth, cols], (q, zrow, cols)) for q in blocks]
        else:
            ends = [(d.at[q, rows, cols], (q, rows, cols)) for q in blocks]
        return [(rc(f"h{m}{s}{h}{i}", src, b.at[i], dev), b.at[i], into)
                for i, (src, into) in enumerate(ends) if only is None or i == only]

    def add_hop(m, s, h, only=None):
        for cp, landed, (q, rows, cols) in hop(m, s, h, only):
            got(cp)
            if h < 2:
                parts[m][q, rows, cols] += landed[...]
            else:
                landed[...] += parts[m][q, rows, cols]
        if h == 2:
            go(*gives(m, s))
            for cp in stores(m, s):
                cp.start()

    def fin_rows(m, s, other=False):
        split = ORDERS[m][s][2] != "Z"
        base = s * FC + (c * HID if m == 1 else 0)
        if split:
            base = base + ((1 - z) if other else z) * ROWS
        return pl.ds(pl.multiple_of(base, ROWS), ROWS if split else FC)

    def cols_c(q):
        return pl.ds(pl.multiple_of(q * 256, 256), 256)

    def gives(m, s):
        b, split = buf[m, s, 2], ORDERS[m][s][2] != "Z"
        rows = fin_rows(m, s)
        if m == 2:
            return [rc(f"a2{s}", b.at[0], d2_out.at[rows, :], dev_z)] if split else []
        out = [rc(f"c1{s}", b.at[0, :, cols_c(1 - c)], d1_out.at[rows, :], dev_c)]
        if split:
            out += [rc(f"a1{s}", b.at[0, :, cols_c(c)], d1_out.at[rows, :], dev_z),
                    rc(f"k1{s}", b.at[0, :, cols_c(1 - c)], d1_out.at[rows, :], dev_zc)]
        return out

    def stores(m, s):
        b = buf[m, s, 2]
        if m == 2:
            return [pltpu.make_async_copy(b.at[0], d2_out.at[fin_rows(m, s), :], loc.at[4 + s])]
        return [pltpu.make_async_copy(b.at[0, :, cols_c(c)], d1_out.at[fin_rows(m, s), :], loc.at[s])]

    mine, theirs = pl.ds(0, TOK // 2), pl.ds(TOK // 2, TOK // 2)

    def t_cp(i):
        return rc(f"cp{i}", (yacc, dxacc)[i].at[theirs, :], (yl, dl)[i], dev_c)

    def out_rows(q):
        return pl.ds(pl.multiple_of(q * (TOK // 2), TOK // 2), TOK // 2)

    def t_yo(i):
        cols = (hi, far_cols[0])[i]
        return rc(f"yo{i}", (xs, gs)[i].at[mine, cols], (y_out, dx_out)[i].at[out_rows(y), :], dev_y)

    def l_yo(i):
        cols = (lo, own_cols[0])[i]
        return pltpu.make_async_copy((xs, gs)[i].at[mine, cols], (y_out, dx_out)[i].at[out_rows(y), :], loc.at[8 + i])

    stage = None
    for m, s in ((m, s) for s in range(4) for m in (1, 2)):
        b = buf[m, s, 0]
        if stage is None and b.shape != (2, FC, HALF):
            stage = [b.at[0], b.at[1]] if b.shape[0] == 2 else [b.at[0, pl.ds(0, ROWS)], b.at[0, pl.ds(ROWS, ROWS)]]

    def finish(i):
        got(t_cp(i))
        acc, piece, dst = (yacc, dxacc)[i], (yl, dl)[i], (xs, gs)[i]

        def fetch(q, k):
            rows = pl.ds(pl.multiple_of(q * ROWS, ROWS), ROWS)
            return pltpu.make_async_copy(piece.at[rows, :], stage[k], isem.at[k])
        fetch(0, 0).start()

        def two(p, _):
            for k in (0, 1):
                q = 2 * p + k

                @pl.when(q + 1 < TOK // 2 // ROWS)
                def _():
                    fetch(q + 1, 1 - k).start()
                fetch(q, k).wait()
                rows = pl.ds(pl.multiple_of(q * ROWS, ROWS), ROWS)
                dst[rows, :] = (acc[rows, :] + stage[k][...]).astype(BF16)
            return 0
        lax.fori_loop(0, TOK // 2 // ROWS // 2, two, 0)
        go(t_yo(i))
        l_yo(i).start()

    def event(name):
        kind, a = name.rstrip("0123456789a"), name
        n = int(name[-1]) if name[-1].isdigit() else None
        if kind == "wy":
            go(*wy(n))
        elif kind == "wxo":
            go(*wx(n), *wp(n))
        elif kind == "t":
            go(*ty(n), *tp(n))
            for cp in tl(n):
                cp.start()
        elif kind == "fw":
            got(*wy_in(n))
            go(*wf(n))
        elif kind == "fzx":
            got(*wx_in(n))
            go(*wzx(n))
        elif kind == "fz":
            got(*wf(n))
            go(*wz(n))
        elif kind == "lw":
            if n % 2 == 0:
                got(*wzx(n // 2), *wz(n // 2), *wp(n // 2))
            load_w(n, n % 2, True)
        elif kind == "ft":
            got(*ty(n))
            go(*tf(n))
            for cp in tl(n):
                cp.wait()
        elif kind == "fr":
            got(*tp(n), *tf(n))
        elif kind in ("s", "b"):
            m, s, h = int(a[1]), int(a[2]), int(a[3])
            only = int(a[4]) if len(a) > 4 and a[4] != "a" else None
            if kind == "s":
                go(*[q[0] for q in hop(m, s, h, only)])
            else:
                add_hop(m, s, h, only)
        elif kind == "cp":
            go(t_cp(0), t_cp(1))
            for i in (0, 1):
                for cp in tf(i):
                    cp.wait_send()
        elif kind == "fin":
            finish(n)

    for name in FIRST:
        event(name)

    def zero(i, _):
        rows = pl.ds(pl.multiple_of(i * 64, 64), 64)
        yacc[rows, :] = jnp.zeros((64, HID), F32)
        dxacc[rows, :] = jnp.zeros((64, HID), F32)
        return 0
    lax.fori_loop(0, TOK // 64, zero, 0)

    plan = {n: list(v) for n, v in PLAN.items()}
    plan.setdefault(1, []).append("fr0")
    plan.setdefault(3, []).append("fr1")
    for name in plan[0]:
        event(name)

    def tile(n, _):
        for at in sorted(plan):
            if 0 < at < NCH * NT:
                @pl.when(n == at)
                def _():
                    for name in plan[at]:
                        event(name)
        j, q = n // NT, n % NT
        slot = j % 2

        @pl.when(q == 0)
        def _():
            load_w(j, slot, False)
        w1, w2 = w1s.at[slot], w2s.at[slot]
        t = (q % 2) * 2 + q // 2
        rows = pl.ds(pl.multiple_of(t * TILE, TILE), TILE)
        xt, gt = xs[rows, :], gs[rows, :]
        u = dot(xt, w1[...], 1, 0)
        da = dot(gt, w2[...], 1, 1)
        cdf = 0.5 * (1.0 + lax.erf(u * INV_ROOT_TWO))
        act = (u * cdf).astype(BF16)
        du = (da * (cdf + u * jnp.exp(-0.5 * u * u) * INV_ROOT_TAU)).astype(BF16)
        yacc[rows, :] += dot(act, w2[...], 1, 0)
        dxacc[rows, :] += dot(du, w1[...], 1, 1)
        p2, p1 = dot(act, gt, 0, 0), dot(du, xt, 0, 0)

        @pl.when(q == 0)
        def _():
            d2[j] = p2
            d1[j] = p1

        @pl.when(q > 0)
        def _():
            d2[j] += p2
            d1[j] += p1
        return 0
    lax.fori_loop(0, NCH * NT, tile, 0)
    for name in plan[NCH * NT]:
        event(name)

    for s in range(4):
        for cp in wy(s) + wx(s) + wp(s) + wf(s) + wzx(s) + wz(s):
            cp.wait_send()
        for m in (1, 2):
            for h in range(3):
                for cp, _, _ in hop(m, s, h):
                    cp.wait_send()
            for cp in gives(m, s):
                cp.wait_send()
                cp.wait_recv()
            for cp in stores(m, s):
                cp.wait()
    for i in (0, 1):
        for cp in ty(i) + tp(i) + [t_cp(i), t_yo(i)]:
            cp.wait_send()
        got(t_yo(i))
        l_yo(i).wait()


def fused(tok, grad, up, down):
    any_spec = pl.BlockSpec(memory_space=pl.ANY)
    vm, shape = pltpu.VMEM, jax.ShapeDtypeStruct
    land = [vm(dims, F32) for m in (1, 2) for s in range(4) for dims in hop_shapes(ORDERS[m][s])]
    dma = pltpu.SemaphoreType.DMA
    return pl.pallas_call(
        kernel,
        name="mlp_block",
        out_shape=(shape((TOK, HALF), BF16), shape((TOK, HALF), BF16), shape((2048, 256), F32), shape((1024, HALF), F32),
                   shape((TOK // 2, HID), F32), shape((TOK // 2, HID), F32),
                   shape((2, HID, HID), BF16), shape((2, HID, HID), BF16)),
        in_specs=[any_spec] * 4,
        out_specs=[any_spec] * 8,
        scratch_shapes=[
            vm((TOK, HID), BF16), vm((TOK, HID), BF16), vm((TOK, HID), F32), vm((TOK, HID), F32),
            vm((NCH, FC, HID), F32), vm((NCH, FC, HID), F32), vm((2, HID, FC), BF16), vm((2, FC, HID), BF16),
            dma((160,)), dma((160,)), dma((10,)), dma((2, 5)), dma((4,)), *land,
        ],
        compiler_params=pltpu.CompilerParams(collective_id=0, has_side_effects=True, vmem_limit_bytes=67_043_328),
    )(tok, grad, up, down)


def solution(mesh):
    act_spec = P(("depth", "row"), "col")
    wgt_spec = P("row", "col")

    def block(tok, up, down, grad):
        out = fused(tok, grad, up, down)
        return out[0], out[1], out[2].T, out[3]

    return jax.shard_map(block, mesh=mesh, in_specs=(act_spec, wgt_spec, wgt_spec, act_spec),
                         out_specs=(act_spec, act_spec, wgt_spec, wgt_spec), check_vma=False)
```

time: 1080 us -> 245 us (0.23)
  waiting for transfers between devices: 961 us -> 0 us
  Pallas kernels: 0 us -> 235 us
  matrix products: 97.3 us -> 0 us
  between operations: 13.9 us -> 0.65 us
    reduce_scatter x4 -> x0, waiting for transfers between devices: 579 us -> none  [the longest x1 369 us: grid_block(): lax.psum_scatter(act_part, 'col', scatter_dimension=1, tiled=True)]
    all_gather x4 -> x0, waiting for transfers between devices: 292 us -> none  [the longest x1 183 us: grid_block(): act_rows = lax.all_gather(hidden_act, 'col', axis=1, tiled=True)]
    pallas_call x0 -> x1, Pallas kernels: none -> 235 us  [fused(): pl.pallas_call(kernel, name='mlp_block', out_shape=(shape((TOK, HALF), BF...]
    dot_general x6 -> x0, matrix products: 97.3 us -> none  [the longest x1 22.4 us: grid_block(): jnp.einsum('th,hf->tf', tok_rows, up_cols, preferred_element_type=jnp.flo...]
    psum x1 -> x0, waiting for transfers between devices: 88 us -> none  [grid_block(): lax.psum(lax.psum_scatter(up_part, 'row', scatter_dimension=0, tiled=True...]
  transfers between devices with their start and end apart: 9 -> 0, of which waited for: 9 -> 0; matrix products, arithmetic and copies ran while one was open for 7% -> 0% of each run, Pallas kernels for 0% -> 0%
where the time goes in v2:
time: 245 us; the launch traced here: 244 us
  Pallas kernels  235 us (96%)
  local copies, waits for them, and re-layouts  9.05 us (4%)
    pallas_call x1, Pallas kernels, fused(): pl.pallas_call(kernel, name='mlp_block', out_shape=(shape((TOK, HALF), BF...  235 us
    unnamed x10, local copies, waits for them, and re-layouts  9.05 us

profile of v2, /device:TPU:0, one launch (start us, length us, event | category | flops | bytes accessed | tf_op | source)
XLA Modules:
  0.0 244.4 jit_solution(13347098329769888098)
XLA Ops:
  0.6 234.7 %mlp_block.1 = (bf16[2048,512]{1,0:T(8,128)(2,1)}, bf16[2048,512]{1,0:T(8,128)(2,1)}, f32[2048,256]{1,0:T(8,128)}, f32[1024,512]{1,0:T(8,128)}, f32[1024,1024]{1...) custom-call(bf16[2048,512]{1,0:T(8,128)(2,1)} %x_in.1, ...), custom_call_target="tpu_custom_call" | custom-call | tf_op jit(solution)/shard_map/mlp_block/pallas_call | solution.py:456
  235.3 0.0 copy-start.2
  235.3 3.0 %copy.8 = f32[256,2048]{1,0:T(8,128)} copy(f32[256,2048]{0,1:T(8,128)} %bitcast.1) | data formatting | bytes 4194304
  238.4 0.0 copy-done.2
  238.4 0.0 copy-start.1
  238.4 1.3 copy.12
  239.7 1.0 copy-done.1
  240.7 0.0 copy-start
  240.7 1.3 copy.13
  242.0 1.0 copy-done
  243.1 1.3 copy.14
Async XLA Ops:
  235.3 3.0 %copy-start.2 = (bf16[2048,512]{1,0:T(8,128)(2,1)S(1)}, bf16[2048,512]{1,0:T(8,128)(2,1)}, u32[]{:S(2)}) copy-start(bf16[2048,512]{1,0:T(8,128)(2,1)} %get-tuple-element.20) | copy-start | bytes 6291460
  238.4 2.3 copy-start.1
  240.7 2.3 copy-start

commit v3 on v2

--- a/solution.py
+++ b/solution.py
@@ -14,32 +14,40 @@
 TOK, HID, FC, NCH = 2048, 1024, 256, 8
 HALF, TILE, ROWS = 512, 512, 128
 NT = TOK // TILE
-FIRST = ("wy0", "t0", "wy1", "t1", "wy2", "wy3", "wxo0", "wxo1", "wxo2", "wxo3",)
-ORDERS = {1: ("ZCB", "CZB", "CBZ", "CZB"),
-          2: ("CZB", "CBZ", "CBZ", "ZBC")}
+ROUTES = "BAAB"
+ORDERS = {1: ("CBZ", "ZBC", "ZCB", "BCZ"),
+          2: ("CBZ", "CBZ", "BZC", "BZC")}
 PLAN = {
-    0: ("fw0", "fzx0", "fzx1", "fzx2", "fzx3", "ft0", "fz0", "fw1", "fz1", "lw0", "lw1",),
-    2: ("ft1",),
-    4: ("fw2", "lw2", "s1000", "s2000",),
-    6: ("fw3",),
-    8: ("fz2", "lw3", "s1001", "s2001",),
-    10: ("fz3", "b1000",),
+    0: ("gwxo0", "gwy1", "gwxo1", "gwy0", "gwxo2", "gt0", "fzx0", "fw1", "gwzx0", "gwxf1", "fzx1", "fw0",
+        "gwz0", "gwzx1", "gwxo3", "fzx2", "gwzx2", "fz0", "gwxf0", "fz1", "gwz1", "gt1", "fzx3", "ft0",
+        "gwzx3", "lw0", "lw1",),
+    2: ("gwy2", "gwy3", "ft1",),
+    4: ("fw2", "lw2", "gwxf2", "gh2000",),
+    5: ("gh1000",),
+    6: ("fw3", "gwz3",),
+    8: ("fz2", "lw3", "gh2001", "gwz2",),
+    9: ("gh1001",),
+    10: ("fz3",),
     11: ("b2000",),
-    12: ("s1100", "s2100",),
-    15: ("lw4", "b2001", "s201",),
-    16: ("lw5", "s1101", "s2101",),
-    18: ("b1100",),
-    19: ("b1001", "s101",),
-    20: ("s1200", "s2200", "b2100",),
-    22: ("b1101", "s111",),
-    23: ("lw6",),
-    24: ("lw7", "s1201", "s2201", "b2101", "s211",),
-    26: ("b101", "s102",),
-    28: ("s1300", "s2300", "b201", "b2200", "s202",),
-    31: ("b1200",),
-    32: ("cp", "s1301", "s2301", "b111", "s112", "b2201", "s221", "b102", "b1201", "s121", "b2300", "fin0",
-        "b112", "b211", "s212", "fin1", "b2301", "b121", "s231", "s122", "b1300", "b202", "b212", "b1301",
-        "s131", "b122", "b221", "s222", "b231", "s232", "b131", "s132", "b232", "b132", "b222",),
+    12: ("b1000", "gh2100", "gh1100",),
+    14: ("lw4", "gwxf3",),
+    15: ("b2001",),
+    16: ("lw5", "gh1101",),
+    17: ("b1001", "gh101",),
+    18: ("gh201",),
+    19: ("b1100",),
+    20: ("b2100", "gh1200",),
+    21: ("lw6", "gh2101",),
+    23: ("b1101",),
+    24: ("lw7", "b101", "gh2200",),
+    25: ("gh102",),
+    26: ("b201", "gh111",),
+    28: ("b1200",),
+    29: ("b2101", "gh202",),
+    32: ("cp", "gh2300", "gh1300", "b102", "b111", "gh1201", "b2200", "fin00", "b202", "fin01", "gh221",
+        "gyo01", "fin10", "fin11", "b1201", "gh112", "b1300", "gh211", "gyo11", "b2300", "gh231", "b221",
+        "b112", "ga11", "gh121", "gh222", "b231", "gh232", "b211", "gh212", "gh131", "gyo10", "b222",
+        "ga22", "b121", "b232", "ga23", "b212", "gh122", "gyo00", "b131", "gh132", "b122", "ga12", "b132",),
 }
 
 def dot(a, b, ca, cb):
@@ -142,7 +150,11 @@
     def wp(s):
         return [rc(f"wp{s}", up_in.at[:, up_cols(1 - c, s)], w1b.at[y, chunk(c), chunk(s)], dev_c)]
 
-    def wf(s):
+    def wxf(s):
+        if ROUTES[s] == "B":
+            both = w2b.at[x, chunk(s), hi]
+            return [rc(f"wf{s}0", w1b.at[1 - y, lo, chunk(s)], w1b.at[1 - y, hi, chunk(s)], dev_x),
+                    rc(f"wF{s}", both, both, dev_x)]
         two = [rc(f"wf{s}{q}", w1b.at[1 - y, part(0, q, z), chunk(s)], w1b.at[1 - y, part(1, q, z), chunk(s)], dev_x)
                for q in (0, 1)]
         both = w2b.at[x, down_rows(s), hi]
@@ -156,6 +168,9 @@
             same_z(f"wzX{s}", w2b.at[1 - x, down_rows(s), lo])]
 
     def wz(s):
+        if ROUTES[s] == "B":
+            return [same_z(f"wz{s}0{q}", w1b.at[1 - y, part(0, q, z), chunk(s)]) for q in (0, 1)] + [
+                same_z(f"wZ{s}0", w2b.at[x, down_rows(s), hi])]
         return [same_z(f"wz{s}{h}{q}", w1b.at[1 - y, part(h, q, z), chunk(s)]) for h in (0, 1) for q in (0, 1)] + [
             same_z(f"wZ{s}{i}", w2b.at[(x, 1 - x)[i], down_rows(s), hi]) for i in (0, 1)]
 
@@ -250,7 +265,7 @@
             else:
                 landed[...] += parts[m][q, rows, cols]
         if h == 2:
-            go(*gives(m, s))
+            go(*gives(m, s, False))
             for cp in stores(m, s):
                 cp.start()
 
@@ -264,16 +279,17 @@
     def cols_c(q):
         return pl.ds(pl.multiple_of(q * 256, 256), 256)
 
-    def gives(m, s):
+    def gives(m, s, far):
         b, split = buf[m, s, 2], ORDERS[m][s][2] != "Z"
         rows = fin_rows(m, s)
+        if far and not split or m == 2 and not far:
+            return []
         if m == 2:
-            return [rc(f"a2{s}", b.at[0], d2_out.at[rows, :], dev_z)] if split else []
-        out = [rc(f"c1{s}", b.at[0, :, cols_c(1 - c)], d1_out.at[rows, :], dev_c)]
-        if split:
-            out += [rc(f"a1{s}", b.at[0, :, cols_c(c)], d1_out.at[rows, :], dev_z),
-                    rc(f"k1{s}", b.at[0, :, cols_c(1 - c)], d1_out.at[rows, :], dev_zc)]
-        return out
+            return [rc(f"a2{s}", b.at[0], d2_out.at[rows, :], dev_z)]
+        if not far:
+            return [rc(f"c1{s}", b.at[0, :, cols_c(1 - c)], d1_out.at[rows, :], dev_c)]
+        return [rc(f"a1{s}", b.at[0, :, cols_c(c)], d1_out.at[rows, :], dev_z),
+                rc(f"k1{s}", b.at[0, :, cols_c(1 - c)], d1_out.at[rows, :], dev_zc)]
 
     def stores(m, s):
         b = buf[m, s, 2]
@@ -286,16 +302,16 @@
     def t_cp(i):
         return rc(f"cp{i}", (yacc, dxacc)[i].at[theirs, :], (yl, dl)[i], dev_c)
 
-    def out_rows(q):
-        return pl.ds(pl.multiple_of(q * (TOK // 2), TOK // 2), TOK // 2)
-
-    def t_yo(i):
-        cols = (hi, far_cols[0])[i]
-        return rc(f"yo{i}", (xs, gs)[i].at[mine, cols], (y_out, dx_out)[i].at[out_rows(y), :], dev_y)
-
-    def l_yo(i):
-        cols = (lo, own_cols[0])[i]
-        return pltpu.make_async_copy((xs, gs)[i].at[mine, cols], (y_out, dx_out)[i].at[out_rows(y), :], loc.at[8 + i])
+    def out_rows(k):
+        return pl.ds(pl.multiple_of(y * (TOK // 2) + k * HALF, HALF), HALF)
+
+    def t_yo(i, k):
+        return rc(f"yo{i}{k}", (xs, gs)[i].at[pl.ds(k * HALF, HALF), (hi, far_cols[0])[i]],
+                  (y_out, dx_out)[i].at[out_rows(k), :], dev_y)
+
+    def l_yo(i, k):
+        return pltpu.make_async_copy((xs, gs)[i].at[pl.ds(k * HALF, HALF), (lo, own_cols[0])[i]],
+                                     (y_out, dx_out)[i].at[out_rows(k), :], loc.at[8 + 2 * i + k])
 
     stage = None
     for m, s in ((m, s) for s in range(4) for m in (1, 2)):
@@ -303,53 +319,62 @@
         if stage is None and b.shape != (2, FC, HALF):
             stage = [b.at[0], b.at[1]] if b.shape[0] == 2 else [b.at[0, pl.ds(0, ROWS)], b.at[0, pl.ds(ROWS, ROWS)]]
 
-    def finish(i):
-        got(t_cp(i))
+    def finish(i, half):
+        if half == 0:
+            got(t_cp(i))
         acc, piece, dst = (yacc, dxacc)[i], (yl, dl)[i], (xs, gs)[i]
 
+        def rows_of(q):
+            return pl.ds(pl.multiple_of(half * HALF + q * ROWS, ROWS), ROWS)
+
         def fetch(q, k):
-            rows = pl.ds(pl.multiple_of(q * ROWS, ROWS), ROWS)
-            return pltpu.make_async_copy(piece.at[rows, :], stage[k], isem.at[k])
+            return pltpu.make_async_copy(piece.at[rows_of(q), :], stage[k], isem.at[k])
         fetch(0, 0).start()
 
         def two(p, _):
             for k in (0, 1):
                 q = 2 * p + k
 
-                @pl.when(q + 1 < TOK // 2 // ROWS)
+                @pl.when(q + 1 < HALF // ROWS)
                 def _():
                     fetch(q + 1, 1 - k).start()
                 fetch(q, k).wait()
-                rows = pl.ds(pl.multiple_of(q * ROWS, ROWS), ROWS)
+                rows = rows_of(q)
                 dst[rows, :] = (acc[rows, :] + stage[k][...]).astype(BF16)
             return 0
-        lax.fori_loop(0, TOK // 2 // ROWS // 2, two, 0)
-        go(t_yo(i))
-        l_yo(i).start()
+        lax.fori_loop(0, HALF // ROWS // 2, two, 0)
+        l_yo(i, half).start()
 
     def event(name):
-        kind, a = name.rstrip("0123456789a"), name
-        n = int(name[-1]) if name[-1].isdigit() else None
-        if kind == "wy":
+        kind, a = name.rstrip("0123456789"), name.lstrip("abcdefghijklmnopqrstuvwxyz")
+        n = int(a[0]) if a else 0
+        hop_of = [int(q) for q in a[:3]] + [int(a[3]) if len(a) > 3 else None]
+        if kind == "gwy":
             go(*wy(n))
-        elif kind == "wxo":
+        elif kind == "gwxo":
             go(*wx(n), *wp(n))
-        elif kind == "t":
+        elif kind == "gt":
             go(*ty(n), *tp(n))
             for cp in tl(n):
                 cp.start()
+        elif kind in ("gwxf", "gwzx", "gwz"):
+            go(*{"gwxf": wxf, "gwzx": wzx, "gwz": wz}[kind](n))
+        elif kind == "gh":
+            go(*[q[0] for q in hop(*hop_of)])
+        elif kind == "ga":
+            go(*gives(n, int(a[1]), True))
+        elif kind == "gyo":
+            go(t_yo(n, int(a[1])))
         elif kind == "fw":
             got(*wy_in(n))
-            go(*wf(n))
         elif kind == "fzx":
             got(*wx_in(n))
-            go(*wzx(n))
         elif kind == "fz":
-            got(*wf(n))
-            go(*wz(n))
+            got(*(wz(n) if ROUTES[n] == "B" else wxf(n)))
         elif kind == "lw":
             if n % 2 == 0:
-                got(*wzx(n // 2), *wz(n // 2), *wp(n // 2))
+                s = n // 2
+                got(*wzx(s), *(wxf(s) if ROUTES[s] == "B" else wz(s)), *wp(s))
             load_w(n, n % 2, True)
         elif kind == "ft":
             got(*ty(n))
@@ -358,35 +383,29 @@
                 cp.wait()
         elif kind == "fr":
             got(*tp(n), *tf(n))
-        elif kind in ("s", "b"):
-            m, s, h = int(a[1]), int(a[2]), int(a[3])
-            only = int(a[4]) if len(a) > 4 and a[4] != "a" else None
-            if kind == "s":
-                go(*[q[0] for q in hop(m, s, h, only)])
-            else:
-                add_hop(m, s, h, only)
+        elif kind == "b":
+            add_hop(*hop_of)
         elif kind == "cp":
             go(t_cp(0), t_cp(1))
             for i in (0, 1):
                 for cp in tf(i):
                     cp.wait_send()
         elif kind == "fin":
-            finish(n)
-
-    for name in FIRST:
-        event(name)
+            finish(n, int(a[1]))
 
     def zero(i, _):
         rows = pl.ds(pl.multiple_of(i * 64, 64), 64)
         yacc[rows, :] = jnp.zeros((64, HID), F32)
         dxacc[rows, :] = jnp.zeros((64, HID), F32)
         return 0
-    lax.fori_loop(0, TOK // 64, zero, 0)
-
     plan = {n: list(v) for n, v in PLAN.items()}
     plan.setdefault(1, []).append("fr0")
     plan.setdefault(3, []).append("fr1")
-    for name in plan[0]:
+    first = [q for q in range(len(plan[0])) if plan[0][q][0] != "g"][0]
+    for name in plan[0][:first]:
+        event(name)
+    lax.fori_loop(0, TOK // 64, zero, 0)
+    for name in plan[0][first:]:
         event(name)
 
     def tile(n, _):
@@ -430,22 +449,23 @@
         event(name)
 
     for s in range(4):
-        for cp in wy(s) + wx(s) + wp(s) + wf(s) + wzx(s) + wz(s):
+        for cp in wy(s) + wx(s) + wp(s) + wxf(s) + wzx(s) + wz(s):
             cp.wait_send()
         for m in (1, 2):
             for h in range(3):
                 for cp, _, _ in hop(m, s, h):
                     cp.wait_send()
-            for cp in gives(m, s):
+            for cp in gives(m, s, False) + gives(m, s, True):
                 cp.wait_send()
                 cp.wait_recv()
             for cp in stores(m, s):
                 cp.wait()
     for i in (0, 1):
-        for cp in ty(i) + tp(i) + [t_cp(i), t_yo(i)]:
+        for cp in ty(i) + tp(i) + [t_cp(i), t_yo(i, 0), t_yo(i, 1)]:
             cp.wait_send()
-        got(t_yo(i))
-        l_yo(i).wait()
+        for k in (0, 1):
+            got(t_yo(i, k))
+            l_yo(i, k).wait()
 
 
 def fused(tok, grad, up, down):
@@ -464,7 +484,7 @@
         scratch_shapes=[
             vm((TOK, HID), BF16), vm((TOK, HID), BF16), vm((TOK, HID), F32), vm((TOK, HID), F32),
             vm((NCH, FC, HID), F32), vm((NCH, FC, HID), F32), vm((2, HID, FC), BF16), vm((2, FC, HID), BF16),
-            dma((160,)), dma((160,)), dma((10,)), dma((2, 5)), dma((4,)), *land,
+            dma((160,)), dma((160,)), dma((12,)), dma((2, 5)), dma((4,)), *land,
         ],
         compiler_params=pltpu.CompilerParams(collective_id=0, has_side_effects=True, vmem_limit_bytes=67_043_328),
     )(tok, grad, up, down)

time: 245 us -> 239 us (0.976)
  Pallas kernels: 235 us -> 229 us
    pallas_call x1, Pallas kernels: 235 us -> 229 us  [fused(): pl.pallas_call(kernel, name='mlp_block', out_shape=(shape((TOK, HALF), BF...]
where the time goes in v3:
time: 239 us
  Pallas kernels  229 us (96%)
  local copies, waits for them, and re-layouts  9.05 us (4%)
    pallas_call x1, Pallas kernels, fused(): pl.pallas_call(kernel, name='mlp_block', out_shape=(shape((TOK, HALF), BF...  229 us
    unnamed x10, local copies, waits for them, and re-layouts  9.05 us

profile of v3, /device:TPU:0, one launch (start us, length us, event | category | flops | bytes accessed | tf_op | source)
XLA Modules:
  0.0 238.9 jit_solution(414443771709534413)
XLA Ops:
  0.6 229.2 %mlp_block.1 = (bf16[2048,512]{1,0:T(8,128)(2,1)}, bf16[2048,512]{1,0:T(8,128)(2,1)}, f32[2048,256]{1,0:T(8,128)}, f32[1024,512]{1,0:T(8,128)}, f32[1024,1024]{1...) custom-call(bf16[2048,512]{1,0:T(8,128)(2,1)} %x_in.1, ...), custom_call_target="tpu_custom_call" | custom-call | tf_op jit(solution)/shard_map/mlp_block/pallas_call | solution.py:476
  229.9 0.0 copy-start.2
  229.9 3.0 %copy.8 = f32[256,2048]{1,0:T(8,128)} copy(f32[256,2048]{0,1:T(8,128)} %bitcast.1) | data formatting | bytes 4194304
  232.9 0.0 copy-done.2
  232.9 0.0 copy-start.1
  232.9 1.3 copy.12
  234.2 1.0 copy-done.1
  235.3 0.0 copy-start
  235.3 1.3 copy.13
  236.6 1.0 copy-done
  237.6 1.3 copy.14
Async XLA Ops:
  229.9 3.0 %copy-start.2 = (bf16[2048,512]{1,0:T(8,128)(2,1)S(1)}, bf16[2048,512]{1,0:T(8,128)(2,1)}, u32[]{:S(2)}) copy-start(bf16[2048,512]{1,0:T(8,128)(2,1)} %get-tuple-element.20) | copy-start | bytes 6291460
  232.9 2.3 copy-start.1
  235.3 2.3 copy-start

commit v4 on v3

--- a/solution.py
+++ b/solution.py
@@ -490,13 +490,35 @@
     )(tok, grad, up, down)
 
 
+def settle_kernel(y_in, dx_in, d1_in, d2_in, y_ref, dx_ref, d1_ref, d2_ref):
+    y_ref[...] = y_in[...]
+    dx_ref[...] = dx_in[...]
+    d1_ref[...] = d1_in[...].T
+    d2_ref[...] = d2_in[...]
+
+
+def settle(y, dx, d1t, d2):
+    steps = 2
+    shape = jax.ShapeDtypeStruct
+
+    def rows(n, cols):
+        return pl.BlockSpec((n // steps, cols), lambda i: (i, 0))
+    return pl.pallas_call(
+        settle_kernel,
+        name="settle",
+        grid=(steps,),
+        out_shape=(shape(y.shape, BF16), shape(dx.shape, BF16), shape(d1t.shape[::-1], F32), shape(d2.shape, F32)),
+        in_specs=[rows(TOK, HALF), rows(TOK, HALF), rows(2048, 256), rows(1024, HALF)],
+        out_specs=[rows(TOK, HALF), rows(TOK, HALF), pl.BlockSpec((256, 2048 // steps), lambda i: (0, i)), rows(1024, HALF)],
+    )(y, dx, d1t, d2)
+
+
 def solution(mesh):
     act_spec = P(("depth", "row"), "col")
     wgt_spec = P("row", "col")
 
     def block(tok, up, down, grad):
-        out = fused(tok, grad, up, down)
-        return out[0], out[1], out[2].T, out[3]
+        return settle(*fused(tok, grad, up, down)[:4])
 
     return jax.shard_map(block, mesh=mesh, in_specs=(act_spec, wgt_spec, wgt_spec, act_spec),
                          out_specs=(act_spec, act_spec, wgt_spec, wgt_spec), check_vma=False)

time: 239 us -> 236 us (0.987)
  local copies, waits for them, and re-layouts: 9.05 us -> 0 us
  Pallas kernels: 229 us -> 235 us
    unnamed x10 -> x0, local copies, waits for them, and re-layouts: 9.05 us -> none
    pallas_call x0 -> x1, Pallas kernels: none -> 5.83 us  [settle(): pl.pallas_call(settle_kernel, name='settle', grid=(steps,), out_shape=(sh...]
where the time goes in v4:
time: 236 us
  Pallas kernels  235 us (100%)
    pallas_call x1, Pallas kernels, fused(): pl.pallas_call(kernel, name='mlp_block', out_shape=(shape((TOK, HALF), BF...  229 us
    pallas_call x1, Pallas kernels, settle(): pl.pallas_call(settle_kernel, name='settle', grid=(steps,), out_shape=(sh...  5.83 us

profile of v4, /device:TPU:0, one launch (start us, length us, event | category | flops | bytes accessed | tf_op | source)
XLA Modules:
  0.0 235.7 jit_solution(5812591131842423951)
XLA Ops:
  0.6 229.2 %mlp_block.1 = (bf16[2048,512]{1,0:T(8,128)(2,1)}, bf16[2048,512]{1,0:T(8,128)(2,1)}, f32[2048,256]{1,0:T(8,128)}, f32[1024,512]{1,0:T(8,128)}, f32[1024,1024]{1...) custom-call(bf16[2048,512]{1,0:T(8,128)(2,1)} %x_in.1, ...), custom_call_target="tpu_custom_call" | custom-call | tf_op jit(solution)/shard_map/mlp_block/pallas_call | solution.py:476
  229.9 5.8 %settle.1 = (bf16[2048,512]{1,0:T(8,128)(2,1)}, bf16[2048,512]{1,0:T(8,128)(2,1)}, f32[256,2048]{1,0:T(8,128)}, f32[1024,512]{1,0:T(8,128)}) custom-call(bf16[2048,512]{1,0:T(8,128)(2,1)} %get-tuple-element.8.y_in, bf16[2048,512]{1,0:T(8,128)(2,1)} %get-tuple-element.9.dx_in, f32[2048,256]{1,0:T(8,128)} %get-tuple-element.10.d1_in, ...), custom_call_target="tpu_custom_call" | custom-call | tf_op jit(solution)/shard_map/settle/pallas_call | solution.py:506

commit v5 on v4

--- a/solution.py
+++ b/solution.py
@@ -12,42 +12,50 @@
 BF16, F32 = jnp.bfloat16, jnp.float32
 
 TOK, HID, FC, NCH = 2048, 1024, 256, 8
-HALF, TILE, ROWS = 512, 512, 128
+HALF, TILE, ROWS, SMALL = 512, 512, 128, 64
 NT = TOK // TILE
 ROUTES = "BAAB"
-ORDERS = {1: ("CBZ", "ZBC", "ZCB", "BCZ"),
-          2: ("CBZ", "CBZ", "BZC", "BZC")}
+ORDERS = {1: ("ZBC", "CBZ", "BZC", "CBZ", "CBZ", "BZC", "ZCB", "CZB"),
+          2: ("CZB", "CBZ", "BZC", "ZBC", "BZC", "CZB", "BCZ", "BCZ")}
 PLAN = {
     0: ("gwxo0", "gwy1", "gwxo1", "gwy0", "gwxo2", "gt0", "fzx0", "fw1", "gwzx0", "gwxf1", "fzx1", "fw0",
         "gwz0", "gwzx1", "gwxo3", "fzx2", "gwzx2", "fz0", "gwxf0", "fz1", "gwz1", "gt1", "fzx3", "ft0",
         "gwzx3", "lw0", "lw1",),
     2: ("gwy2", "gwy3", "ft1",),
-    4: ("fw2", "lw2", "gwxf2", "gh2000",),
-    5: ("gh1000",),
+    4: ("fw2", "lw2", "gwxf2", "gh2000", "gh1000",),
+    5: ("gh1100", "gh2100",),
     6: ("fw3", "gwz3",),
-    8: ("fz2", "lw3", "gh2001", "gwz2",),
-    9: ("gh1001",),
-    10: ("fz3",),
-    11: ("b2000",),
-    12: ("b1000", "gh2100", "gh1100",),
-    14: ("lw4", "gwxf3",),
-    15: ("b2001",),
-    16: ("lw5", "gh1101",),
-    17: ("b1001", "gh101",),
-    18: ("gh201",),
-    19: ("b1100",),
-    20: ("b2100", "gh1200",),
-    21: ("lw6", "gh2101",),
-    23: ("b1101",),
-    24: ("lw7", "b101", "gh2200",),
-    25: ("gh102",),
-    26: ("b201", "gh111",),
-    28: ("b1200",),
-    29: ("b2101", "gh202",),
-    32: ("cp", "gh2300", "gh1300", "b102", "b111", "gh1201", "b2200", "fin00", "b202", "fin01", "gh221",
-        "gyo01", "fin10", "fin11", "b1201", "gh112", "b1300", "gh211", "gyo11", "b2300", "gh231", "b221",
-        "b112", "ga11", "gh121", "gh222", "b231", "gh232", "b211", "gh212", "gh131", "gyo10", "b222",
-        "ga22", "b121", "b232", "ga23", "b212", "gh122", "gyo00", "b131", "gh132", "b122", "ga12", "b132",),
+    8: ("fz2", "lw3", "b1000", "b2000", "gh1101", "gh2101", "gwz2",),
+    10: ("fz3", "b1100", "gwxf3", "gh2001",),
+    11: ("b2100",),
+    12: ("b1101", "gh111", "gh2300",),
+    13: ("b2101",),
+    14: ("gh1300", "gh1001",),
+    15: ("lw4", "b2001",),
+    16: ("lw5", "gh1301", "gh1200", "gh2301", "b2300",),
+    17: ("b111",),
+    18: ("gh2200", "gh112",),
+    19: ("b1300", "b1001", "gh101",),
+    20: ("lw6", "gh201",),
+    21: ("b1301", "b2301", "gh131",),
+    22: ("b1200", "gh1400", "gh121",),
+    23: ("b112", "gh2500",),
+    24: ("lw7", "b101",),
+    25: ("b2200", "b201", "gh2400", "gh1500", "gh221",),
+    26: ("b131",),
+    27: ("gh132",),
+    28: ("b1400", "b121", "b2500",),
+    29: ("gh1401", "gh1600",),
+    30: ("b221", "gh222",),
+    31: ("gh1700", "gh2501",),
+    32: ("cp", "b2400", "b132", "gh241", "b1500", "gh2600", "gh1601", "b222", "b1401", "b1600", "gh141",
+        "ga22", "b2501", "b1700", "b241", "gh242", "fin00", "gyo00", "gh251", "fin01", "b141", "gh2700",
+        "b1601", "gh142", "b242", "fin10", "fin11", "b2600", "gh261", "ga24", "b251", "gh252", "gh151",
+        "gyo10", "gh1701", "b142", "b2700", "gh161", "b261", "gh262", "b252", "ga25", "gh271", "b151",
+        "gh152", "b1701", "gh171", "gh122", "gyo01", "b262", "gh231", "b161", "b152", "ga15", "gh102",
+        "b271", "gh272", "b122", "b171", "gh202", "ga12", "gh162", "gh211", "gh172", "b231", "gh232",
+        "b102", "b272", "ga10", "gyo11", "b202", "ga20", "b162", "ga16", "b172", "ga17", "b211", "gh212",
+        "b232", "ga23", "b212",),
 }
 
 def dot(a, b, ca, cb):
@@ -55,14 +63,14 @@
 
 
 def hop_shapes(order):
-    nb, rows, cols, shapes = 2, FC, HID, []
+    nb, rows, cols, shapes = 2, ROWS, HID, []
     for h, kind in enumerate(order):
         if kind == "B":
             nb = 1
         elif kind == "C":
             cols = HALF
         elif h < 2:
-            rows = ROWS
+            rows = ROWS // 2
         shapes.append((nb, rows, cols))
     return shapes
 
@@ -227,34 +235,38 @@
                                       isem.at[2 * i + k]) for k in (0, 1)]
 
     parts = {1: d1, 2: d2}
-    buf = {(m, s, h): land[(m - 1) * 12 + s * 3 + h] for m in (1, 2) for s in range(4) for h in range(3)}
+    buf = {(m, u, h): land[(m - 1) * 24 + u * 3 + h] for m in (1, 2) for u in range(8) for h in range(3)}
     keep_block = {1: y, 2: x}
     dev_of = {(1, "C"): dev_x, (1, "B"): dev_y, (1, "Z"): dev_z, (2, "C"): dev_y, (2, "B"): dev_x, (2, "Z"): dev_z}
 
-    def live(m, s, h):
-        blocks, rows, cols = [2 * s, 2 * s + 1], everything, everything
-        for kind in ORDERS[m][s][:h]:
+    def z_rows(u, zi):
+        return pl.ds(pl.multiple_of(u % 2 * ROWS + zi * (ROWS // 2), ROWS // 2), ROWS // 2)
+
+    def live(m, u, h):
+        first = u // 2 * 2
+        blocks, rows, cols = [first, first + 1], pl.ds(u % 2 * ROWS, ROWS), everything
+        for kind in ORDERS[m][u][:h]:
             if kind == "B":
-                blocks = [2 * s + keep_block[m]]
+                blocks = [first + keep_block[m]]
             elif kind == "C":
                 cols = lo
             else:
-                rows = zrow
+                rows = z_rows(u, z)
         return blocks, rows, cols
 
-    def hop(m, s, h, only=None):
-        kind = ORDERS[m][s][h]
-        blocks, rows, cols = live(m, s, h)
-        d, b, dev = parts[m], buf[m, s, h], dev_of[m, kind]
+    def hop(m, u, h, only=None):
+        kind = ORDERS[m][u][h]
+        blocks, rows, cols = live(m, u, h)
+        d, b, dev, first = parts[m], buf[m, u, h], dev_of[m, kind], u // 2 * 2
         if kind == "B":
-            ends = [(d.at[2 * s + 1 - keep_block[m], rows, cols], (2 * s + keep_block[m], rows, cols))]
+            ends = [(d.at[first + 1 - keep_block[m], rows, cols], (first + keep_block[m], rows, cols))]
         elif kind == "C":
             ends = [(d.at[q, rows, hi], (q, rows, lo)) for q in blocks]
         elif h < 2:
-            ends = [(d.at[q, zoth, cols], (q, zrow, cols)) for q in blocks]
+            ends = [(d.at[q, z_rows(u, 1 - z), cols], (q, z_rows(u, z), cols)) for q in blocks]
         else:
             ends = [(d.at[q, rows, cols], (q, rows, cols)) for q in blocks]
-        return [(rc(f"h{m}{s}{h}{i}", src, b.at[i], dev), b.at[i], into)
+        return [(rc(f"h{m}{u}{h}{i}", src, b.at[i], dev), b.at[i], into)
                 for i, (src, into) in enumerate(ends) if only is None or i == only]
 
     def add_hop(m, s, h, only=None):
@@ -269,12 +281,12 @@
             for cp in stores(m, s):
                 cp.start()
 
-    def fin_rows(m, s, other=False):
-        split = ORDERS[m][s][2] != "Z"
-        base = s * FC + (c * HID if m == 1 else 0)
+    def fin_rows(m, u):
+        split = ORDERS[m][u][2] != "Z"
+        base = u * ROWS + (c * HID if m == 1 else 0)
         if split:
-            base = base + ((1 - z) if other else z) * ROWS
-        return pl.ds(pl.multiple_of(base, ROWS), ROWS if split else FC)
+            base = base + z * (ROWS // 2)
+        return pl.ds(pl.multiple_of(base, ROWS // 2), ROWS // 2 if split else ROWS)
 
     def cols_c(q):
         return pl.ds(pl.multiple_of(q * 256, 256), 256)
@@ -294,7 +306,7 @@
     def stores(m, s):
         b = buf[m, s, 2]
         if m == 2:
-            return [pltpu.make_async_copy(b.at[0], d2_out.at[fin_rows(m, s), :], loc.at[4 + s])]
+            return [pltpu.make_async_copy(b.at[0], d2_out.at[fin_rows(m, s), :], loc.at[8 + s])]
         return [pltpu.make_async_copy(b.at[0, :, cols_c(c)], d1_out.at[fin_rows(m, s), :], loc.at[s])]
 
     mine, theirs = pl.ds(0, TOK // 2), pl.ds(TOK // 2, TOK // 2)
@@ -311,13 +323,13 @@
 
     def l_yo(i, k):
         return pltpu.make_async_copy((xs, gs)[i].at[pl.ds(k * HALF, HALF), (lo, own_cols[0])[i]],
-                                     (y_out, dx_out)[i].at[out_rows(k), :], loc.at[8 + 2 * i + k])
+                                     (y_out, dx_out)[i].at[out_rows(k), :], loc.at[16 + 2 * i + k])
 
     stage = None
-    for m, s in ((m, s) for s in range(4) for m in (1, 2)):
-        b = buf[m, s, 0]
-        if stage is None and b.shape != (2, FC, HALF):
-            stage = [b.at[0], b.at[1]] if b.shape[0] == 2 else [b.at[0, pl.ds(0, ROWS)], b.at[0, pl.ds(ROWS, ROWS)]]
+    for m, u in ((m, u) for u in range(8) for m in (1, 2)):
+        b = buf[m, u, 0]
+        if stage is None and b.shape != (2, ROWS, HALF):
+            stage = [b.at[0], b.at[1]] if b.shape[0] == 2 else [b.at[0, pl.ds(k * SMALL, SMALL)] for k in (0, 1)]
 
     def finish(i, half):
         if half == 0:
@@ -325,7 +337,7 @@
         acc, piece, dst = (yacc, dxacc)[i], (yl, dl)[i], (xs, gs)[i]
 
         def rows_of(q):
-            return pl.ds(pl.multiple_of(half * HALF + q * ROWS, ROWS), ROWS)
+            return pl.ds(pl.multiple_of(half * HALF + q * SMALL, SMALL), SMALL)
 
         def fetch(q, k):
             return pltpu.make_async_copy(piece.at[rows_of(q), :], stage[k], isem.at[k])
@@ -335,14 +347,14 @@
             for k in (0, 1):
                 q = 2 * p + k
 
-                @pl.when(q + 1 < HALF // ROWS)
+                @pl.when(q + 1 < HALF // SMALL)
                 def _():
                     fetch(q + 1, 1 - k).start()
                 fetch(q, k).wait()
                 rows = rows_of(q)
                 dst[rows, :] = (acc[rows, :] + stage[k][...]).astype(BF16)
             return 0
-        lax.fori_loop(0, HALF // ROWS // 2, two, 0)
+        lax.fori_loop(0, HALF // SMALL // 2, two, 0)
         l_yo(i, half).start()
 
     def event(name):
@@ -451,15 +463,15 @@
     for s in range(4):
         for cp in wy(s) + wx(s) + wp(s) + wxf(s) + wzx(s) + wz(s):
             cp.wait_send()
-        for m in (1, 2):
-            for h in range(3):
-                for cp, _, _ in hop(m, s, h):
-                    cp.wait_send()
-            for cp in gives(m, s, False) + gives(m, s, True):
+    for m, u in ((m, u) for m in (1, 2) for u in range(8)):
+        for h in range(3):
+            for cp, _, _ in hop(m, u, h):
                 cp.wait_send()
-                cp.wait_recv()
-            for cp in stores(m, s):
-                cp.wait()
+        for cp in gives(m, u, False) + gives(m, u, True):
+            cp.wait_send()
+            cp.wait_recv()
+        for cp in stores(m, u):
+            cp.wait()
     for i in (0, 1):
         for cp in ty(i) + tp(i) + [t_cp(i), t_yo(i, 0), t_yo(i, 1)]:
             cp.wait_send()
@@ -471,7 +483,7 @@
 def fused(tok, grad, up, down):
     any_spec = pl.BlockSpec(memory_space=pl.ANY)
     vm, shape = pltpu.VMEM, jax.ShapeDtypeStruct
-    land = [vm(dims, F32) for m in (1, 2) for s in range(4) for dims in hop_shapes(ORDERS[m][s])]
+    land = [vm(dims, F32) for m in (1, 2) for u in range(8) for dims in hop_shapes(ORDERS[m][u])]
     dma = pltpu.SemaphoreType.DMA
     return pl.pallas_call(
         kernel,
@@ -484,7 +496,7 @@
         scratch_shapes=[
             vm((TOK, HID), BF16), vm((TOK, HID), BF16), vm((TOK, HID), F32), vm((TOK, HID), F32),
             vm((NCH, FC, HID), F32), vm((NCH, FC, HID), F32), vm((2, HID, FC), BF16), vm((2, FC, HID), BF16),
-            dma((160,)), dma((160,)), dma((12,)), dma((2, 5)), dma((4,)), *land,
+            dma((250,)), dma((250,)), dma((20,)), dma((2, 5)), dma((4,)), *land,
         ],
         compiler_params=pltpu.CompilerParams(collective_id=0, has_side_effects=True, vmem_limit_bytes=67_043_328),
     )(tok, grad, up, down)

time: 236 us -> 234 us (level)
  no operation moved by 1% of the time
where the time goes in v5:
time: 234 us; the launch traced here: 233 us
  Pallas kernels  233 us (100%)
    pallas_call x1, Pallas kernels, fused(): pl.pallas_call(kernel, name='mlp_block', out_shape=(shape((TOK, HALF), BF...  227 us
    pallas_call x1, Pallas kernels, settle(): pl.pallas_call(settle_kernel, name='settle', grid=(steps,), out_shape=(sh...  5.83 us

profile of v5, /device:TPU:0, one launch (start us, length us, event | category | flops | bytes accessed | tf_op | source)
XLA Modules:
  0.0 233.4 jit_solution(2826676459541742238)
XLA Ops:
  0.6 226.9 %mlp_block.1 = (bf16[2048,512]{1,0:T(8,128)(2,1)}, bf16[2048,512]{1,0:T(8,128)(2,1)}, f32[2048,256]{1,0:T(8,128)}, f32[1024,512]{1,0:T(8,128)}, f32[1024,1024]{1...) custom-call(bf16[2048,512]{1,0:T(8,128)(2,1)} %x_in.1, ...), custom_call_target="tpu_custom_call" | custom-call | tf_op jit(solution)/shard_map/mlp_block/pallas_call | solution.py:488
  227.6 5.8 %settle.1 = (bf16[2048,512]{1,0:T(8,128)(2,1)}, bf16[2048,512]{1,0:T(8,128)(2,1)}, f32[256,2048]{1,0:T(8,128)}, f32[1024,512]{1,0:T(8,128)}) custom-call(bf16[2048,512]{1,0:T(8,128)(2,1)} %get-tuple-element.8.y_in, bf16[2048,512]{1,0:T(8,128)(2,1)} %get-tuple-element.9.dx_in, f32[2048,256]{1,0:T(8,128)} %get-tuple-element.10.d1_in, ...), custom_call_target="tpu_custom_call" | custom-call | tf_op jit(solution)/shard_map/settle/pallas_call | solution.py:518

commit v6 on v5

--- a/solution.py
+++ b/solution.py
@@ -14,48 +14,48 @@
 TOK, HID, FC, NCH = 2048, 1024, 256, 8
 HALF, TILE, ROWS, SMALL = 512, 512, 128, 64
 NT = TOK // TILE
-ROUTES = "BAAB"
-ORDERS = {1: ("ZBC", "CBZ", "BZC", "CBZ", "CBZ", "BZC", "ZCB", "CZB"),
-          2: ("CZB", "CBZ", "BZC", "ZBC", "BZC", "CZB", "BCZ", "BCZ")}
+GWY, GWXO, GT, GWXF, GWZX, GWZ, GH, GA, GYO, FW, FZX, FZ, LW, FT, FR, BH, CP, FIN = range(18)
+ROUTES = "ABBA"
+ORDERS = {1: ("CZB", "ZCB", "CBZ", "ZBC", "CZB", "ZCB", "ZBC", "CBZ"),
+          2: ("CBZ", "CBZ", "BZC", "CBZ", "BCZ", "CBZ", "CBZ", "BZC")}
 PLAN = {
-    0: ("gwxo0", "gwy1", "gwxo1", "gwy0", "gwxo2", "gt0", "fzx0", "fw1", "gwzx0", "gwxf1", "fzx1", "fw0",
-        "gwz0", "gwzx1", "gwxo3", "fzx2", "gwzx2", "fz0", "gwxf0", "fz1", "gwz1", "gt1", "fzx3", "ft0",
-        "gwzx3", "lw0", "lw1",),
-    2: ("gwy2", "gwy3", "ft1",),
-    4: ("fw2", "lw2", "gwxf2", "gh2000", "gh1000",),
-    5: ("gh1100", "gh2100",),
-    6: ("fw3", "gwz3",),
-    8: ("fz2", "lw3", "b1000", "b2000", "gh1101", "gh2101", "gwz2",),
-    10: ("fz3", "b1100", "gwxf3", "gh2001",),
-    11: ("b2100",),
-    12: ("b1101", "gh111", "gh2300",),
-    13: ("b2101",),
-    14: ("gh1300", "gh1001",),
-    15: ("lw4", "b2001",),
-    16: ("lw5", "gh1301", "gh1200", "gh2301", "b2300",),
-    17: ("b111",),
-    18: ("gh2200", "gh112",),
-    19: ("b1300", "b1001", "gh101",),
-    20: ("lw6", "gh201",),
-    21: ("b1301", "b2301", "gh131",),
-    22: ("b1200", "gh1400", "gh121",),
-    23: ("b112", "gh2500",),
-    24: ("lw7", "b101",),
-    25: ("b2200", "b201", "gh2400", "gh1500", "gh221",),
-    26: ("b131",),
-    27: ("gh132",),
-    28: ("b1400", "b121", "b2500",),
-    29: ("gh1401", "gh1600",),
-    30: ("b221", "gh222",),
-    31: ("gh1700", "gh2501",),
-    32: ("cp", "b2400", "b132", "gh241", "b1500", "gh2600", "gh1601", "b222", "b1401", "b1600", "gh141",
-        "ga22", "b2501", "b1700", "b241", "gh242", "fin00", "gyo00", "gh251", "fin01", "b141", "gh2700",
-        "b1601", "gh142", "b242", "fin10", "fin11", "b2600", "gh261", "ga24", "b251", "gh252", "gh151",
-        "gyo10", "gh1701", "b142", "b2700", "gh161", "b261", "gh262", "b252", "ga25", "gh271", "b151",
-        "gh152", "b1701", "gh171", "gh122", "gyo01", "b262", "gh231", "b161", "b152", "ga15", "gh102",
-        "b271", "gh272", "b122", "b171", "gh202", "ga12", "gh162", "gh211", "gh172", "b231", "gh232",
-        "b102", "b272", "ga10", "gyo11", "b202", "ga20", "b162", "ga16", "b172", "ga17", "b211", "gh212",
-        "b232", "ga23", "b212",),
+    0: (110000, 10001, 110001, 10000, 110002, 210000, 1010000, 910001, 510001, 410000, 110003, 1010001,
+        910000, 410001, 1110001, 310000, 1010002, 410002, 310001, 1010003, 410003, 210001, 1110000, 510000,
+        1310000, 1210000, 1210001, 10002,),
+    2: (10003, 1310001,),
+    4: (910002, 1210002, 641000, 642100, 510002,),
+    5: (641100,),
+    6: (910003, 310003, 642000,),
+    8: (1110002, 1210003, 1541000, 310002, 642101, 641101,),
+    9: (1542100,),
+    10: (1110003, 1541100, 642001, 510003,),
+    11: (1542000,),
+    12: (1541101, 641200, 642300,),
+    13: (1542101,),
+    14: (641001, 641300,),
+    15: (1210004, 1542001,),
+    16: (1210005, 642200, 642301, 641301,),
+    17: (1541200, 1542300,),
+    19: (1541001, 1541300, 630101,),
+    20: (1210006, 1542301, 641201, 642500, 641500,),
+    21: (1541301, 630131,),
+    23: (1542200, 1530101, 641400, 630102, 630221,),
+    24: (1210007, 1542500, 642501,),
+    25: (641401, 641501,),
+    26: (1541201, 1541500, 1530131, 630121,),
+    27: (1530102, 642400, 720010,),
+    28: (1541400, 1530221, 641600,),
+    29: (1542501, 642600,),
+    30: (1541401, 1541501, 630141,),
+    31: (630222,),
+    32: (1600000, 1530121, 641700, 642601, 630122, 1541600, 1542600, 642700, 1542400, 630241, 1530222,
+        720022, 1530141, 641601, 630142, 1720000, 1541700, 1542601, 1720001, 1530122, 641701, 820000,
+        1530241, 630242, 1720010, 1530142, 630201, 720014, 1720011, 1542700, 1541601, 630271, 630161,
+        630261, 1541701, 1530242, 630171, 630151, 1530201, 630202, 820011, 1530271, 630211, 1530161,
+        1530261, 630262, 1530202, 630162, 1530171, 630172, 1530151, 630132, 630272, 1530262, 630111,
+        630152, 1530211, 630212, 820001, 1530162, 720016, 1530172, 630231, 1530132, 720013, 1530272,
+        720027, 1530212, 1530152, 630251, 720015, 1530111, 630112, 820010, 1530231, 630232, 1530251,
+        630252, 1530112, 720011, 1530232, 1530252,),
 }
 
 def dot(a, b, ca, cb):
@@ -357,53 +357,57 @@
         lax.fori_loop(0, HALF // SMALL // 2, two, 0)
         l_yo(i, half).start()
 
-    def event(name):
-        kind, a = name.rstrip("0123456789"), name.lstrip("abcdefghijklmnopqrstuvwxyz")
-        n = int(a[0]) if a else 0
-        hop_of = [int(q) for q in a[:3]] + [int(a[3]) if len(a) > 3 else None]
-        if kind == "gwy":
+    def event(code):
+        kind, count = code // 100000, code // 10000 % 10
+        args = [code // 10**k % 10 for k in reversed(range(count))]
+        n = args[0] if args else 0
+        if kind == GWY:
             go(*wy(n))
-        elif kind == "gwxo":
+        elif kind == GWXO:
             go(*wx(n), *wp(n))
-        elif kind == "gt":
+        elif kind == GT:
             go(*ty(n), *tp(n))
             for cp in tl(n):
                 cp.start()
-        elif kind in ("gwxf", "gwzx", "gwz"):
-            go(*{"gwxf": wxf, "gwzx": wzx, "gwz": wz}[kind](n))
-        elif kind == "gh":
-            go(*[q[0] for q in hop(*hop_of)])
-        elif kind == "ga":
-            go(*gives(n, int(a[1]), True))
-        elif kind == "gyo":
-            go(t_yo(n, int(a[1])))
-        elif kind == "fw":
+        elif kind == GWXF:
+            go(*wxf(n))
+        elif kind == GWZX:
+            go(*wzx(n))
+        elif kind == GWZ:
+            go(*wz(n))
+        elif kind == GH:
+            go(*[q[0] for q in hop(*args)])
+        elif kind == GA:
+            go(*gives(*args, True))
+        elif kind == GYO:
+            go(t_yo(*args))
+        elif kind == FW:
             got(*wy_in(n))
-        elif kind == "fzx":
+        elif kind == FZX:
             got(*wx_in(n))
-        elif kind == "fz":
+        elif kind == FZ:
             got(*(wz(n) if ROUTES[n] == "B" else wxf(n)))
-        elif kind == "lw":
+        elif kind == LW:
             if n % 2 == 0:
                 s = n // 2
                 got(*wzx(s), *(wxf(s) if ROUTES[s] == "B" else wz(s)), *wp(s))
             load_w(n, n % 2, True)
-        elif kind == "ft":
+        elif kind == FT:
             got(*ty(n))
             go(*tf(n))
             for cp in tl(n):
                 cp.wait()
-        elif kind == "fr":
+        elif kind == FR:
             got(*tp(n), *tf(n))
-        elif kind == "b":
-            add_hop(*hop_of)
-        elif kind == "cp":
+        elif kind == BH:
+            add_hop(*args)
+        elif kind == CP:
             go(t_cp(0), t_cp(1))
             for i in (0, 1):
                 for cp in tf(i):
                     cp.wait_send()
-        elif kind == "fin":
-            finish(n, int(a[1]))
+        elif kind == FIN:
+            finish(*args)
 
     def zero(i, _):
         rows = pl.ds(pl.multiple_of(i * 64, 64), 64)
@@ -411,9 +415,9 @@
         dxacc[rows, :] = jnp.zeros((64, HID), F32)
         return 0
     plan = {n: list(v) for n, v in PLAN.items()}
-    plan.setdefault(1, []).append("fr0")
-    plan.setdefault(3, []).append("fr1")
-    first = [q for q in range(len(plan[0])) if plan[0][q][0] != "g"][0]
+    plan.setdefault(1, []).append(FR * 100000 + 10000)
+    plan.setdefault(3, []).append(FR * 100000 + 10001)
+    first = [q for q in range(len(plan[0])) if plan[0][q] // 100000 > GYO][0]
     for name in plan[0][:first]:
         event(name)
     lax.fori_loop(0, TOK // 64, zero, 0)

time: 234 us -> 234 us (level)
  no operation moved by 1% of the time
where the time goes in v6:
time: 234 us; the launch traced here: 233 us
  Pallas kernels  233 us (100%)
    pallas_call x1, Pallas kernels, fused(): pl.pallas_call(kernel, name='mlp_block', out_shape=(shape((TOK, HALF), BF...  227 us
    pallas_call x1, Pallas kernels, settle(): pl.pallas_call(settle_kernel, name='settle', grid=(steps,), out_shape=(sh...  5.83 us

profile of v6, /device:TPU:0, one launch (start us, length us, event | category | flops | bytes accessed | tf_op | source)
XLA Modules:
  0.0 233.2 jit_solution(15945427394169326212)
XLA Ops:
  0.6 226.7 %mlp_block.1 = (bf16[2048,512]{1,0:T(8,128)(2,1)}, bf16[2048,512]{1,0:T(8,128)(2,1)}, f32[2048,256]{1,0:T(8,128)}, f32[1024,512]{1,0:T(8,128)}, f32[1024,1024]{1...) custom-call(bf16[2048,512]{1,0:T(8,128)(2,1)} %x_in.1, ...), custom_call_target="tpu_custom_call" | custom-call | tf_op jit(solution)/shard_map/mlp_block/pallas_call | solution.py:492
  227.4 5.8 %settle.1 = (bf16[2048,512]{1,0:T(8,128)(2,1)}, bf16[2048,512]{1,0:T(8,128)(2,1)}, f32[256,2048]{1,0:T(8,128)}, f32[1024,512]{1,0:T(8,128)}) custom-call(bf16[2048,512]{1,0:T(8,128)(2,1)} %get-tuple-element.8.y_in, bf16[2048,512]{1,0:T(8,128)(2,1)} %get-tuple-element.9.dx_in, f32[2048,256]{1,0:T(8,128)} %get-tuple-element.10.d1_in, ...), custom_call_target="tpu_custom_call" | custom-call | tf_op jit(solution)/shard_map/settle/pallas_call | solution.py:522

commit v7 on v6

--- a/solution.py
+++ b/solution.py
@@ -18,45 +18,49 @@
 ROUTES = "ABBA"
 ORDERS = {1: ("CZB", "ZCB", "CBZ", "ZBC", "CZB", "ZCB", "ZBC", "CBZ"),
           2: ("CBZ", "CBZ", "BZC", "CBZ", "BCZ", "CBZ", "CBZ", "BZC")}
-PLAN = {
-    0: (110000, 10001, 110001, 10000, 110002, 210000, 1010000, 910001, 510001, 410000, 110003, 1010001,
-        910000, 410001, 1110001, 310000, 1010002, 410002, 310001, 1010003, 410003, 210001, 1110000, 510000,
-        1310000, 1210000, 1210001, 10002,),
-    2: (10003, 1310001,),
-    4: (910002, 1210002, 641000, 642100, 510002,),
-    5: (641100,),
-    6: (910003, 310003, 642000,),
-    8: (1110002, 1210003, 1541000, 310002, 642101, 641101,),
-    9: (1542100,),
-    10: (1110003, 1541100, 642001, 510003,),
-    11: (1542000,),
-    12: (1541101, 641200, 642300,),
-    13: (1542101,),
-    14: (641001, 641300,),
-    15: (1210004, 1542001,),
-    16: (1210005, 642200, 642301, 641301,),
-    17: (1541200, 1542300,),
-    19: (1541001, 1541300, 630101,),
-    20: (1210006, 1542301, 641201, 642500, 641500,),
-    21: (1541301, 630131,),
-    23: (1542200, 1530101, 641400, 630102, 630221,),
-    24: (1210007, 1542500, 642501,),
-    25: (641401, 641501,),
-    26: (1541201, 1541500, 1530131, 630121,),
-    27: (1530102, 642400, 720010,),
-    28: (1541400, 1530221, 641600,),
-    29: (1542501, 642600,),
-    30: (1541401, 1541501, 630141,),
-    31: (630222,),
-    32: (1600000, 1530121, 641700, 642601, 630122, 1541600, 1542600, 642700, 1542400, 630241, 1530222,
-        720022, 1530141, 641601, 630142, 1720000, 1541700, 1542601, 1720001, 1530122, 641701, 820000,
-        1530241, 630242, 1720010, 1530142, 630201, 720014, 1720011, 1542700, 1541601, 630271, 630161,
-        630261, 1541701, 1530242, 630171, 630151, 1530201, 630202, 820011, 1530271, 630211, 1530161,
-        1530261, 630262, 1530202, 630162, 1530171, 630172, 1530151, 630132, 630272, 1530262, 630111,
-        630152, 1530211, 630212, 820001, 1530162, 720016, 1530172, 630231, 1530132, 720013, 1530272,
-        720027, 1530212, 1530152, 630251, 720015, 1530111, 630112, 820010, 1530231, 630232, 1530251,
-        630252, 1530112, 720011, 1530232, 1530252,),
-}
+PLAN = (
+    (110000, 10001, 110001, 10000, 110002, 210000, 1010000, 910001, 510001, 410000, 110003, 1010001, 910000,
+     410001, 1110001, 310000, 1010002, 410002, 310001, 1010003, 410003, 210001, 1110000, 510000, 1310000,
+     1210000, 1210001, 10002,),
+    (),
+    (10003, 1310001,),
+    (),
+    (910002, 1210002, 641000, 642100, 510002,),
+    (641100,),
+    (910003, 310003, 642000,),
+    (),
+    (1110002, 1210003, 1541000, 310002, 642101, 641101,),
+    (1542100,),
+    (1110003, 1541100, 642001, 510003,),
+    (1542000,),
+    (1541101, 641200, 642300,),
+    (1542101,),
+    (641001, 641300,),
+    (1210004, 1542001,),
+    (1210005, 642200, 642301, 641301,),
+    (1541200, 1542300,),
+    (),
+    (1541001, 1541300, 630101,),
+    (1210006, 1542301, 641201, 642500, 641500,),
+    (1541301, 630131,),
+    (),
+    (1542200, 1530101, 641400, 630102, 630221,),
+    (1210007, 1542500, 642501,),
+    (641401, 641501,),
+    (1541201, 1541500, 1530131, 630121,),
+    (1530102, 642400, 720010,),
+    (1541400, 1530221, 641600,),
+    (1542501, 642600,),
+    (1541401, 1541501, 630141,),
+    (630222,),
+    (1600000, 1530121, 641700, 642601, 630122, 1541600, 1542600, 642700, 1542400, 630241, 1530222, 720022,
+     1530141, 641601, 630142, 1720000, 1541700, 1542601, 1720001, 1530122, 641701, 820000, 1530241, 630242,
+     1720010, 1530142, 630201, 720014, 1720011, 1542700, 1541601, 630271, 630161, 630261, 1541701, 1530242,
+     630171, 630151, 1530201, 630202, 820011, 1530271, 630211, 1530161, 1530261, 630262, 1530202, 630162,
+     1530171, 630172, 1530151, 630132, 630272, 1530262, 630111, 630152, 1530211, 630212, 820001, 1530162,
+     720016, 1530172, 630231, 1530132, 720013, 1530272, 720027, 1530212, 1530152, 630251, 720015, 1530111,
+     630112, 820010, 1530231, 630232, 1530251, 630252, 1530112, 720011, 1530232, 1530252,),
+)
 
 def dot(a, b, ca, cb):
     return lax.dot_general(a, b, (((ca,), (cb,)), ((), ())), preferred_element_type=F32)
@@ -135,25 +139,25 @@
 
     def wy(s):
         two = [by_core("wy", s, q, up_in.at[zrow, up_cols(q, s)], w1b.at[y, part(0, c, z), chunk(s)], (z, 1 - y, x * 2 + q))
-               for q in (0, 1)]
+               for q in range(2)]
         return two + [wy_down(s)]
 
     def wy_down(s):
         return rc(f"wY{s}", down_in.at[down_rows(s), :], w2b.at[x, down_rows(s), hi], dev_y)
 
     def wy_in(s):
-        return [by_core_in("wy", s, q, w1b.at[1 - y, part(0, q, z), chunk(s)]) for q in (0, 1)] + [wy_down(s)]
+        return [by_core_in("wy", s, q, w1b.at[1 - y, part(0, q, z), chunk(s)]) for q in range(2)] + [wy_down(s)]
 
     def wx(s):
         two = [by_core("wx", s, q, up_in.at[zrow, up_cols(q, s)], w1b.at[y, part(1, c, z), chunk(s)],
-                       (z, y, (1 - x) * 2 + q)) for q in (0, 1)]
+                       (z, y, (1 - x) * 2 + q)) for q in range(2)]
         return two + [wx_down(s)]
 
     def wx_down(s):
         return rc(f"wX{s}", down_in.at[down_rows(s), :], w2b.at[x, down_rows(s), lo], dev_x)
 
     def wx_in(s):
-        return [by_core_in("wx", s, q, w1b.at[y, part(1, q, z), chunk(s)]) for q in (0, 1)] + [wx_down(s)]
+        return [by_core_in("wx", s, q, w1b.at[y, part(1, q, z), chunk(s)]) for q in range(2)] + [wx_down(s)]
 
     def wp(s):
         return [rc(f"wp{s}", up_in.at[:, up_cols(1 - c, s)], w1b.at[y, chunk(c), chunk(s)], dev_c)]
@@ -164,7 +168,7 @@
             return [rc(f"wf{s}0", w1b.at[1 - y, lo, chunk(s)], w1b.at[1 - y, hi, chunk(s)], dev_x),
                     rc(f"wF{s}", both, both, dev_x)]
         two = [rc(f"wf{s}{q}", w1b.at[1 - y, part(0, q, z), chunk(s)], w1b.at[1 - y, part(1, q, z), chunk(s)], dev_x)
-               for q in (0, 1)]
+               for q in range(2)]
         both = w2b.at[x, down_rows(s), hi]
         return two + [rc(f"wF{s}", both, both, dev_x)]
 
@@ -172,15 +176,15 @@
         return rc(name, ref, ref, dev_z)
 
     def wzx(s):
-        return [same_z(f"wzx{s}{q}", w1b.at[y, part(1, q, z), chunk(s)]) for q in (0, 1)] + [
+        return [same_z(f"wzx{s}{q}", w1b.at[y, part(1, q, z), chunk(s)]) for q in range(2)] + [
             same_z(f"wzX{s}", w2b.at[1 - x, down_rows(s), lo])]
 
     def wz(s):
         if ROUTES[s] == "B":
-            return [same_z(f"wz{s}0{q}", w1b.at[1 - y, part(0, q, z), chunk(s)]) for q in (0, 1)] + [
+            return [same_z(f"wz{s}0{q}", w1b.at[1 - y, part(0, q, z), chunk(s)]) for q in range(2)] + [
                 same_z(f"wZ{s}0", w2b.at[x, down_rows(s), hi])]
-        return [same_z(f"wz{s}{h}{q}", w1b.at[1 - y, part(h, q, z), chunk(s)]) for h in (0, 1) for q in (0, 1)] + [
-            same_z(f"wZ{s}{i}", w2b.at[(x, 1 - x)[i], down_rows(s), hi]) for i in (0, 1)]
+        return [same_z(f"wz{s}{h}{q}", w1b.at[1 - y, part(h, q, z), chunk(s)]) for h in range(2) for q in range(2)] + [
+            same_z(f"wZ{s}{i}", w2b.at[(x, 1 - x)[i], down_rows(s), hi]) for i in range(2)]
 
     def load_w(j, slot, start):
         s, b = j // 2, j % 2
@@ -221,18 +225,18 @@
 
     def ty(i):
         return [rc(f"ty{i}{k}", ins[k].at[tok_at(1 - y, i), :], tok[k].at[tok_at(0, i), (own_cols[0], hi)[k]], dev_y)
-                for k in (0, 1)]
+                for k in range(2)]
 
     def tp(i):
-        return [rc(f"tp{i}{k}", ins[k].at[tok_at(y, i), :], tok[k].at[tok_at(1, i), own_cols[k]], dev_c) for k in (0, 1)]
+        return [rc(f"tp{i}{k}", ins[k].at[tok_at(y, i), :], tok[k].at[tok_at(1, i), own_cols[k]], dev_c) for k in range(2)]
 
     def tf(i):
         return [rc(f"tf{i}{k}", tok[k].at[tok_at(0, i), far_cols[k]], tok[k].at[tok_at(1, i), far_cols[k]], dev_c)
-                for k in (0, 1)]
+                for k in range(2)]
 
     def tl(i):
         return [pltpu.make_async_copy(ins[k].at[tok_at(y, i), :], tok[k].at[tok_at(0, i), own_cols[k]],
-                                      isem.at[2 * i + k]) for k in (0, 1)]
+                                      isem.at[2 * i + k]) for k in range(2)]
 
     parts = {1: d1, 2: d2}
     buf = {(m, u, h): land[(m - 1) * 24 + u * 3 + h] for m in (1, 2) for u in range(8) for h in range(3)}
@@ -329,7 +333,7 @@
     for m, u in ((m, u) for u in range(8) for m in (1, 2)):
         b = buf[m, u, 0]
         if stage is None and b.shape != (2, ROWS, HALF):
-            stage = [b.at[0], b.at[1]] if b.shape[0] == 2 else [b.at[0, pl.ds(k * SMALL, SMALL)] for k in (0, 1)]
+            stage = [b.at[0], b.at[1]] if b.shape[0] == 2 else [b.at[0, pl.ds(k * SMALL, SMALL)] for k in range(2)]
 
     def finish(i, half):
         if half == 0:
@@ -344,7 +348,7 @@
         fetch(0, 0).start()
 
         def two(p, _):
-            for k in (0, 1):
+            for k in range(2):
                 q = 2 * p + k
 
                 @pl.when(q + 1 < HALF // SMALL)
@@ -403,7 +407,7 @@
             add_hop(*args)
         elif kind == CP:
             go(t_cp(0), t_cp(1))
-            for i in (0, 1):
+            for i in range(2):
                 for cp in tf(i):
                     cp.wait_send()
         elif kind == FIN:
@@ -414,9 +418,9 @@
         yacc[rows, :] = jnp.zeros((64, HID), F32)
         dxacc[rows, :] = jnp.zeros((64, HID), F32)
         return 0
-    plan = {n: list(v) for n, v in PLAN.items()}
-    plan.setdefault(1, []).append(FR * 100000 + 10000)
-    plan.setdefault(3, []).append(FR * 100000 + 10001)
+    plan = [list(v) for v in PLAN]
+    plan[1].append(FR * 100000 + 10000)
+    plan[3].append(FR * 100000 + 10001)
     first = [q for q in range(len(plan[0])) if plan[0][q] // 100000 > GYO][0]
     for name in plan[0][:first]:
         event(name)
@@ -425,8 +429,8 @@
         event(name)
 
     def tile(n, _):
-        for at in sorted(plan):
-            if 0 < at < NCH * NT:
+        for at in range(1, NCH * NT):
+            if plan[at]:
                 @pl.when(n == at)
                 def _():
                     for name in plan[at]:
@@ -476,10 +480,10 @@
             cp.wait_recv()
         for cp in stores(m, u):
             cp.wait()
-    for i in (0, 1):
+    for i in range(2):
         for cp in ty(i) + tp(i) + [t_cp(i), t_yo(i, 0), t_yo(i, 1)]:
             cp.wait_send()
-        for k in (0, 1):
+        for k in range(2):
             got(t_yo(i, k))
             l_yo(i, k).wait()
 

time: 234 us -> 234 us (level)
  no operation moved by 1% of the time
where the time goes in v7:
time: 234 us; the launch traced here: 233 us
  Pallas kernels  233 us (100%)
    pallas_call x1, Pallas kernels, fused(): pl.pallas_call(kernel, name='mlp_block', out_shape=(shape((TOK, HALF), BF...  227 us
    pallas_call x1, Pallas kernels, settle(): pl.pallas_call(settle_kernel, name='settle', grid=(steps,), out_shape=(sh...  5.83 us

profile of v7, /device:TPU:0, one launch (start us, length us, event | category | flops | bytes accessed | tf_op | source)
XLA Modules:
  0.0 233.2 jit_solution(15945427394169326212)
XLA Ops:
  0.6 226.7 %mlp_block.1 = (bf16[2048,512]{1,0:T(8,128)(2,1)}, bf16[2048,512]{1,0:T(8,128)(2,1)}, f32[2048,256]{1,0:T(8,128)}, f32[1024,512]{1,0:T(8,128)}, f32[1024,1024]{1...) custom-call(bf16[2048,512]{1,0:T(8,128)(2,1)} %x_in.1, ...), custom_call_target="tpu_custom_call" | custom-call | tf_op jit(solution)/shard_map/mlp_block/pallas_call | solution.py:496
  227.4 5.8 %settle.1 = (bf16[2048,512]{1,0:T(8,128)(2,1)}, bf16[2048,512]{1,0:T(8,128)(2,1)}, f32[256,2048]{1,0:T(8,128)}, f32[1024,512]{1,0:T(8,128)}) custom-call(bf16[2048,512]{1,0:T(8,128)(2,1)} %get-tuple-element.8.y_in, bf16[2048,512]{1,0:T(8,128)(2,1)} %get-tuple-element.9.dx_in, f32[2048,256]{1,0:T(8,128)} %get-tuple-element.10.d1_in, ...), custom_call_target="tpu_custom_call" | custom-call | tf_op jit(solution)/shard_map/settle/pallas_call | solution.py:526
